TPU v7x, 128 devices: a whole 4x4x4 slice. The times are simulated.
128 devices in a mesh: rep: 1, r: 16 (over y, z), s: 8 (over x, core).
Axes of the slice: x: 4, y: 4, z: 4, core: 2. Of those that a mesh axis runs over, the one named last changes fastest.
Arguments:
- x: bfloat16 [128, 2048, 1024], P(('rep', 'r', 's'))
- dy: bfloat16 [128, 2048, 1024], P(('rep', 'r', 's'))
- w_gate: bfloat16 [2, 1024, 3328], P(None, 's')
- w_up: bfloat16 [2, 1024, 3328], P(None, 's')
- w_down: bfloat16 [2, 3328, 1024], P(None, 's')
- m_w_gate: float32 [2, 1024, 3328], P(None, 's')
- m_w_up: float32 [2, 1024, 3328], P(None, 's')
- m_w_down: float32 [2, 3328, 1024], P(None, 's')
- v_w_gate: float32 [2, 1024, 3328], P(None, 's')
- v_w_up: float32 [2, 1024, 3328], P(None, 's')
- v_w_down: float32 [2, 3328, 1024], P(None, 's')
Outputs:
- output 1: bfloat16 [2, 1024, 3328], P('rep', 's')
- output 2: bfloat16 [2, 1024, 3328], P('rep', 's')
- output 3: bfloat16 [2, 3328, 1024], P('rep', 's')
- output 4: float32 [2, 1024, 3328], P('rep', 's')
- output 5: float32 [2, 1024, 3328], P('rep', 's')
- output 6: float32 [2, 3328, 1024], P('rep', 's')
- output 7: float32 [2, 1024, 3328], P('rep', 's')
- output 8: float32 [2, 1024, 3328], P('rep', 's')
- output 9: float32 [2, 3328, 1024], P('rep', 's')
All inputs are finite; a program needn't handle non-finite values.
Results may differ from a plain program's by a relative error of at most 0.022.
Values are sent between devices in bfloat16 or wider.
A program may use at most 1.5 GiB of HBM per device.

v0:
```python
import jax
import jax.numpy as jnp
from jax import lax
from jax.sharding import PartitionSpec as P

NAMES = ("w_gate", "w_up", "w_down")


def matmul(a, w):
    return jnp.dot(a, w, preferred_element_type=jnp.float32).astype(jnp.bfloat16)


def normed(h):
    wide = h.astype(jnp.float32)
    scale = lax.rsqrt(jnp.mean(wide**2, -1, keepdims=True) + 1e-6)
    return (wide * scale).astype(jnp.bfloat16)


def layer(h, w):
    a = normed(h)
    gate = jnp.dot(a, w["w_gate"], preferred_element_type=jnp.float32)
    up = jnp.dot(a, w["w_up"], preferred_element_type=jnp.float32)
    return h + matmul((jax.nn.silu(gate) * up).astype(jnp.bfloat16), w["w_down"])


def adamw(w, m, v, g):
    m = 0.9 * m + 0.1 * g
    v = 0.95 * v + 0.05 * g * g
    step = m * lax.rsqrt(v + 1e-8) + 0.1 * w
    return (w - 0.02 * step).astype(jnp.bfloat16), m, v


def solution(mesh):
    def fetched(weights, number):
        return {name: lax.all_gather(w[number], "s", axis=0, tiled=True) for name, w in zip(NAMES, weights, strict=True)}

    def summed(term):
        return lax.psum(lax.psum_scatter(term, "s", scatter_dimension=0, tiled=True), "r")

    def step(x, dy, *arrays):
        weights, m, v = (arrays[i : i + 3] for i in (0, 3, 6))
        layers = weights[0].shape[0]
        h, kept = x[0], []
        for number in range(layers):
            kept.append(h)
            h = layer(h, fetched(weights, number))
        by_h, mine = dy[0], [None] * layers
        for number in reversed(range(layers)):
            _, back = jax.vjp(lambda w, h: layer(h, w), fetched(weights, number), kept[number])
            by_w, by_h = back(by_h)
            mine[number] = [summed(by_w[name]) for name in NAMES]
        gradients = [jnp.stack([mine[number][i] for number in range(layers)]).astype(jnp.float32) for i in range(3)]
        new = [adamw(w.astype(jnp.float32), m, v, g) for w, m, v, g in zip(weights, m, v, gradients, strict=True)]
        return tuple(one[which] for which in range(3) for one in new)

    states, cut = P(("rep", "r", "s"), None, None), P(None, "s", None)
    return jax.shard_map(
        step,
        mesh=mesh,
        in_specs=(states, states) + (cut,) * 9,
        out_specs=(P("rep", "s", None),) * 9,
        check_vma=False,
    )
```

profile of v0, /device:TPU:0, one launch (start us, length us, event | category | flops | bytes accessed | tf_op | source)
XLA Modules:
  0.0 816.5 jit_solution(16412468742671066517)
XLA Ops:
  7.2 0.0 all-gather.13.cloned.1.call-start
  7.2 2.8 fusion.88
  10.1 0.0 all-gather.13.cloned.1.call-update
  10.1 0.0 all-gather.15.cloned.1.call-start
  10.1 2.7 fusion.87
  12.9 0.0 all-gather.17.cloned.1.call-start
  12.9 1.3 fusion.86
  14.3 0.0 all-gather.23.cloned.1.call-start
  14.3 0.5 all-gather.23.cloned.1.call-update
  14.8 0.0 all-gather.21.cloned.1.call-start
  14.9 0.5 all-gather.21.cloned.1.call-update
  15.4 0.0 all-gather.19.cloned.1.call-start
  15.5 0.5 all-gather.19.cloned.1.call-update
  16.0 0.0 reduce-scatter.15.cloned.1.call-start
  16.0 6.5 copy.20
  22.6 3.1 fusion.15
  25.7 6.5 copy.21
  32.2 23.4 %all-gather.13.cloned.1.call-done = bf16[1,1024,3328]{2,1,0:T(8,128)(2,1)} async-done(((bf16[1,128,3328]{2,1,0:T(8,128)(2,1)}), bf16[1,1024,3328]{2,1,0:T(8,128)(2,1)}) %all-gather.13.cloned.1.call-update) | async-done | bytes 6815760 | tf_op jit(solution)/shard_map/all_gather | solution.py:35
  55.6 23.2 %fusion.41 = f32[2048,3328]{1,0:T(8,128)} fusion(bf16[1,1024,3328]{2,1,0:T(8,128)(2,1)} %all-gather.13.cloned.1.call-done, bf16[1,2048,1024]{1,2,0:T(8,128)(2,1)} %copy.20, f32[2048]{0:T(1024)S(1)} %add_rsqrt_fusion), kind=kOutput, calls=%fused_computation.59 | convolution fusion | flops 13964935168 | bytes 38281216 | tf_op jit(solution)/shard_map/dot_general | solution.py:21
  78.8 22.1 %all-gather.15.cloned.1.call-done = bf16[1,1024,3328]{2,1,0:T(8,128)(2,1)} async-done(((bf16[1,128,3328]{2,1,0:T(8,128)(2,1)}), bf16[1,1024,3328]{2,1,0:T(8,128)(2,1)}) %all-gather.15.cloned.1.call-update) | async-done | bytes 6815760 | tf_op jit(solution)/shard_map/all_gather | solution.py:35
  100.9 32.1 %multiply_convert_fusion.1 = (bf16[2048,3328]{1,0:T(8,128)(2,1)}, f32[2048,3328]{1,0:T(8,128)}) fusion(f32[2048,3328]{1,0:T(8,128)} %fusion.41, bf16[1,1024,3328]{2,1,0:T(8,128)(2,1)} %all-gather.15.cloned.1.call-done, bf16[1,2048,1024]{1,2,0:T(8,128)(2,1)} %copy.20, f32[2048]{0:T(1024)S(1)} %add_rsqrt_fusion), kind=kOutput, calls=%fused_computation.17 | convolution fusion | flops 14005829632 | bytes 79175680 | tf_op jit(solution)/shard_map/dot_general | solution.py:22
  133.0 13.2 %all-gather.17.cloned.1.call-done = bf16[1,3328,1024]{2,1,0:T(8,128)(2,1)} async-done(((bf16[1,416,1024]{2,1,0:T(8,128)(2,1)}), bf16[1,3328,1024]{2,1,0:T(8,128)(2,1)}) %all-gather.17.cloned.1.call-update) | async-done | bytes 6815760 | tf_op jit(solution)/shard_map/all_gather | solution.py:35
  146.1 22.2 %fusion.19 = (f32[2048]{0:T(1024)S(1)}, bf16[2048,1024]{0,1:T(8,128)(2,1)}) fusion(bf16[2048,3328]{1,0:T(8,128)(2,1)} %get-tuple-element.30, bf16[1,3328,1024]{2,1,0:T(8,128)(2,1)} %all-gather.17.cloned.1.call-done, bf16[1,2048,1024]{1,2,0:T(8,128)(2,1)} %copy.20), kind=kOutput, calls=%fused_computation.37 | convolution fusion | flops 13969127424 | bytes 28844032 | tf_op jit(solution)/shard_map/dot_general | solution.py:10
  168.3 23.0 %all-gather.23.cloned.1.call-done = bf16[1,1024,3328]{2,1,0:T(8,128)(2,1)} async-done(((bf16[1,128,3328]{2,1,0:T(8,128)(2,1)}), bf16[1,1024,3328]{2,1,0:T(8,128)(2,1)}) %all-gather.23.cloned.1.call-update) | async-done | bytes 6815760 | tf_op jit(solution)/shard_map/all_gather | solution.py:35
  191.3 23.5 %fusion.28 = f32[2048,3328]{1,0:T(8,128)} fusion(bf16[1,1024,3328]{2,1,0:T(8,128)(2,1)} %all-gather.23.cloned.1.call-done, bf16[2048,1024]{0,1:T(8,128)(2,1)} %get-tuple-element.33, f32[2048]{0:T(1024)S(1)} %fusion.74), kind=kOutput, calls=%fused_computation.46 | convolution fusion | flops 13964935168 | bytes 38281216 | tf_op jit(solution)/shard_map/jvp()/dot_general | solution.py:22
  214.8 21.6 %all-gather.21.cloned.1.call-done = bf16[1,3328,1024]{2,1,0:T(8,128)(2,1)} async-done(((bf16[1,416,1024]{2,1,0:T(8,128)(2,1)}), bf16[1,3328,1024]{2,1,0:T(8,128)(2,1)}) %all-gather.21.cloned.1.call-update) | async-done | bytes 6815760 | tf_op jit(solution)/shard_map/all_gather | solution.py:35
  236.4 21.0 %convolution_convert_fusion.1 = bf16[2048,3328]{1,0:T(8,128)(2,1)} fusion(bf16[1,3328,1024]{2,1,0:T(8,128)(2,1)} %all-gather.21.cloned.1.call-done, bf16[1,2048,1024]{2,1,0:T(8,128)(2,1)} %param.12), kind=kOutput, calls=%fused_computation.23 | convolution fusion | flops 13965459456 | bytes 24641536 | tf_op jit(solution)/shard_map/transpose(jvp())/dot_general | solution.py:10
  257.4 24.1 %all-gather.19.cloned.1.call-done = bf16[1,1024,3328]{2,1,0:T(8,128)(2,1)} async-done(((bf16[1,128,3328]{2,1,0:T(8,128)(2,1)}), bf16[1,1024,3328]{2,1,0:T(8,128)(2,1)}) %all-gather.19.cloned.1.call-update) | async-done | bytes 6815760 | tf_op jit(solution)/shard_map/all_gather | solution.py:35
  281.5 39.6 %fusion.2 = (bf16[2048,3328]{1,0:T(8,128)(2,1)}, f32[2048,3328]{1,0:T(8,128)}) fusion(f32[2048,3328]{1,0:T(8,128)} %fusion.28, bf16[2048,3328]{1,0:T(8,128)(2,1)} %convolution_convert_fusion.1, bf16[1,1024,3328]{2,1,0:T(8,128)(2,1)} %all-gather.19.cloned.1.call-done, bf16[2048,1024]{0,1:T(8,128)(2,1)} %get-tuple-element.33, f32[2048]{0:T(1024)S(1)} %fusion.74), kind=kOutput, calls=%fused_computation.8 | convolution fusion | flops 14046724096 | bytes 92807168 | tf_op jit(solution)/shard_map/jvp()/dot_general | solution.py:21
  321.1 23.1 %fusion.12 = bf16[2048,1024]{0,1:T(8,128)(2,1)} fusion(bf16[2048,3328]{1,0:T(8,128)(2,1)} %convolution_convert_fusion.1, bf16[1,1024,3328]{2,1,0:T(8,128)(2,1)} %all-gather.23.cloned.1.call-done, f32[2048,3328]{1,0:T(8,128)} %get-tuple-element.35), kind=kOutput, calls=%fused_computation.21 | convolution fusion | flops 13999538176 | bytes 51904512 | tf_op jit(solution)/shard_map/transpose(jvp())/dot_general | solution.py:22
  344.3 21.7 %fusion.21 = (f32[2048]{0:T(1024)S(1)}, bf16[2048,1024]{0,1:T(8,128)(2,1)}) fusion(bf16[2048,1024]{0,1:T(8,128)(2,1)S(1)} %copy-done.5, bf16[2048,1024]{0,1:T(8,128)(2,1)} %fusion.12, bf16[2048,3328]{1,0:T(8,128)(2,1)} %get-tuple-element.34, bf16[1,1024,3328]{2,1,0:T(8,128)(2,1)} %all-gather.19.cloned.1.call-done), kind=kOutput, calls=%fused_computation.39 | convolution fusion | flops 13969127424 | bytes 33038336 | tf_op jit(solution)/shard_map/transpose(jvp())/dot_general | solution.py:21
  366.0 4.9 fusion.44
  370.9 2.0 copy-done.6
  372.9 19.6 %convolution_convert_fusion.2 = bf16[3328,1024]{1,0:T(8,128)(2,1)} fusion(bf16[2048,3328]{1,0:T(8,128)(2,1)} %get-tuple-element.30, bf16[2048,1024]{0,1:T(8,128)(2,1)S(1)} %fusion.44), kind=kOutput, calls=%fused_computation.44 | convolution fusion | flops 13962051584 | bytes 24641536 | tf_op jit(solution)/shard_map/transpose(jvp())/dot_general | solution.py:10
  392.5 0.0 reduce-scatter.15.cloned.1.call-update
  392.5 0.0 reduce-scatter.17.cloned.1.call-start
  392.5 27.6 %fusion.25 = bf16[3328,1024]{1,0:T(8,128)(2,1)} fusion(f32[2048,3328]{1,0:T(8,128)} %fusion.28, bf16[1,2048,1024]{2,1,0:T(8,128)(2,1)} %param.12, f32[2048,3328]{1,0:T(8,128)} %get-tuple-element.35), kind=kOutput, calls=%fused_computation.41 | convolution fusion | flops 14002946048 | bytes 65536000 | tf_op jit(solution)/shard_map/transpose(jvp())/dot_general | solution.py:10
  420.2 0.0 reduce-scatter.11.cloned.1.call-start
  420.3 21.1 %convolution_convert_fusion = bf16[2048,3328]{1,0:T(8,128)(2,1)} fusion(bf16[2048,1024]{0,1:T(8,128)(2,1)} %copy-done.6, bf16[1,3328,1024]{2,1,0:T(8,128)(2,1)} %all-gather.17.cloned.1.call-done), kind=kOutput, calls=%fused_computation.22 | convolution fusion | flops 13965459456 | bytes 24641536 | tf_op jit(solution)/shard_map/transpose(jvp())/dot_general | solution.py:10
  441.3 25.5 %fusion.27 = bf16[1024,3328]{1,0:T(8,128)(2,1)} fusion(bf16[2048,3328]{1,0:T(8,128)(2,1)} %convolution_convert_fusion, f32[2048,3328]{1,0:T(8,128)} %fusion.41, bf16[1,2048,1024]{1,2,0:T(8,128)(2,1)} %copy.20, f32[2048]{0:T(1024)S(1)} %copy-done.19), kind=kOutput, calls=%fused_computation.43 | convolution fusion | flops 14009237504 | bytes 51912704 | tf_op jit(solution)/shard_map/transpose(jvp())/dot_general | solution.py:22
  466.9 0.0 reduce-scatter.13.cloned.1.call-start
  466.9 0.6 copy-done.15
  467.6 25.4 %fusion.26 = bf16[1024,3328]{1,0:T(8,128)(2,1)} fusion(bf16[2048,3328]{1,0:T(8,128)(2,1)} %convolution_convert_fusion.1, bf16[2048,1024]{0,1:T(8,128)(2,1)} %get-tuple-element.33, f32[2048]{0:T(1024)S(1)} %copy-done.15, f32[2048,3328]{1,0:T(8,128)} %get-tuple-element.35), kind=kOutput, calls=%fused_computation.42 | convolution fusion | flops 14009237504 | bytes 51912704 | tf_op jit(solution)/shard_map/transpose(jvp())/dot_general | solution.py:22
  492.9 0.0 reduce-scatter.7.cloned.1.call-start
  493.0 31.2 %fusion.22 = bf16[1024,3328]{1,0:T(8,128)(2,1)} fusion(f32[2048,3328]{1,0:T(8,128)} %fusion.41, f32[2048,3328]{1,0:T(8,128)} %get-tuple-element.31, bf16[2048,3328]{1,0:T(8,128)(2,1)} %convolution_convert_fusion, bf16[1,2048,1024]{1,2,0:T(8,128)(2,1)} %copy.20, f32[2048]{0:T(1024)S(1)} %copy-done.19), kind=kOutput, calls=%fused_computation.40 | convolution fusion | flops 14043316224 | bytes 79175680 | tf_op jit(solution)/shard_map/transpose(jvp())/dot_general | solution.py:21
  524.2 0.0 reduce-scatter.9.cloned.1.call-start
  524.3 21.3 %convolution_convert_fusion.3 = bf16[1024,3328]{1,0:T(8,128)(2,1)} fusion(bf16[2048,3328]{1,0:T(8,128)(2,1)} %get-tuple-element.34, bf16[2048,1024]{0,1:T(8,128)(2,1)} %get-tuple-element.33, f32[2048]{0:T(1024)S(1)} %copy-done.15), kind=kOutput, calls=%fused_computation.45 | convolution fusion | flops 13964935168 | bytes 24649728 | tf_op jit(solution)/shard_map/transpose(jvp())/dot_general | solution.py:21
  545.5 0.0 all-reduce.3.cloned.1.call-start
  545.6 0.0 reduce-scatter.15.cloned.1.call-done
  545.6 0.0 reduce-scatter.17.cloned.1.call-done
  545.7 0.0 reduce-scatter.11.cloned.1.call-done
  545.7 33.5 %reduce-scatter.13.cloned.1.call-done = bf16[128,3328]{1,0:T(8,128)(2,1)} async-done(((bf16[1024,3328]{1,0:T(8,128)(2,1)}), bf16[128,3328]{1,0:T(8,128)(2,1)}) %reduce-scatter.13.cloned.1.call-update) | async-done | bytes 851984 | tf_op jit(solution)/shard_map/reduce_scatter | solution.py:38
  579.2 47.2 %reduce-scatter.7.cloned.1.call-done = bf16[128,3328]{1,0:T(8,128)(2,1)} async-done(((bf16[1024,3328]{1,0:T(8,128)(2,1)}), bf16[128,3328]{1,0:T(8,128)(2,1)}) %reduce-scatter.7.cloned.1.call-update) | async-done | bytes 851984 | tf_op jit(solution)/shard_map/reduce_scatter | solution.py:38
  626.3 47.0 %reduce-scatter.9.cloned.1.call-done = bf16[128,3328]{1,0:T(8,128)(2,1)} async-done(((bf16[1024,3328]{1,0:T(8,128)(2,1)}), bf16[128,3328]{1,0:T(8,128)(2,1)}) %reduce-scatter.9.cloned.1.call-update) | async-done | bytes 851984 | tf_op jit(solution)/shard_map/reduce_scatter | solution.py:38
  673.4 115.6 %all-reduce.3.cloned.1.call-done = (bf16[1,128,3328]{2,1,0:T(8,128)(2,1)}, bf16[1,128,3328]{2,1,0:T(8,128)(2,1)}, bf16[1,128,3328]{2,1,0:T(8,128)(2,1)}, bf16[1,...) async-done(((bf16[1,128,3328]{2,1,0:T(8,128)(2,1)}, bf16[1,128,3328]{2,1,0:T(8,128)(2,1)}, bf16[1,128,3328]{2,1,0:T(8,128)(2,1)}, ...) | async-done | bytes 5111824 | tf_op jit(solution)/shard_map/psum | solution.py:38
  789.0 7.6 fusion.61
  796.6 0.4 copy-done.7
  797.0 1.4 copy-done.8
  798.4 1.0 copy-done.9
  799.4 0.1 copy-done.10
  799.5 0.2 copy-done.11
  799.8 0.2 copy-done.12
  800.0 0.2 copy-done.13
  800.3 9.2 %fusion.53 = (bf16[2,128,3328]{2,1,0:T(8,128)(2,1)}, f32[2,128,3328]{2,1,0:T(8,128)}, f32[2,128,3328]{2,1,0:T(8,128)}, bf16[2,128,3328]{2,1,0:T(8,128)(2,1)}, f3...) fusion(bf16[2,128,3328]{2,1,0:T(8,128)(2,1)S(1)} %copy-done.3, bf16[1,128,3328]{2,1,0:T(8,128)(2,1)S(1)} %copy-done.10, ...), kind=kLoop, calls=%fused_computation.80 | loop fusion | flops 32374784 | bytes 37486592 | tf_op jit(solution)/shard_map/convert_element_type | solution.py:30
  (42 shorter events, 0.2 us)
Async XLA Ops:
  7.2 5.7 copy-start.1
  7.2 48.4 %all-gather.13.cloned.1.call-start = ((), (), s32[]{:S(2)}) async-start(), calls=%async_computation.12 | async-start | bytes 7667712 | tf_op jit(solution)/shard_map/all_gather | solution.py:35
  10.1 90.8 %all-gather.15.cloned.1.call-start = ((), (), s32[]{:S(2)}) async-start(), calls=%async_computation.13 | async-start | bytes 7667712 | tf_op jit(solution)/shard_map/all_gather | solution.py:35
  12.9 133.3 %all-gather.17.cloned.1.call-start = ((), (), s32[]{:S(2)}) async-start(), calls=%async_computation.14 | async-start | bytes 7667712 | tf_op jit(solution)/shard_map/all_gather | solution.py:35
  14.3 177.0 %all-gather.23.cloned.1.call-start = ((), (), s32[]{:S(2)}) async-start(), calls=%async_computation.17 | async-start | bytes 7667712 | tf_op jit(solution)/shard_map/all_gather | solution.py:35
  14.8 221.6 %all-gather.21.cloned.1.call-start = ((), (), s32[]{:S(2)}) async-start(), calls=%async_computation.16 | async-start | bytes 7667712 | tf_op jit(solution)/shard_map/all_gather | solution.py:35
  15.4 266.1 %all-gather.19.cloned.1.call-start = ((), (), s32[]{:S(2)}) async-start(), calls=%async_computation.15 | async-start | bytes 7667712 | tf_op jit(solution)/shard_map/all_gather | solution.py:35
  16.0 529.6 %reduce-scatter.15.cloned.1.call-start = ((), (), s32[]{:S(2)}) async-start(), calls=%async_computation.10 | async-start | bytes 7667712 | tf_op jit(solution)/shard_map/reduce_scatter | solution.py:38
  25.6 75.2 %copy-start.18 = (f32[2048]{0:T(1024)}, f32[2048]{0:T(1024)S(1)}, u32[]{:S(2)}) copy-start(f32[2048]{0:T(1024)S(1)} %add_rsqrt_fusion) | copy-start | bytes 24580
  168.3 46.5 %copy-start.16 = (f32[2048]{0:T(1024)}, f32[2048]{0:T(1024)S(1)}, u32[]{:S(2)}) copy-start(f32[2048]{0:T(1024)S(1)} %get-tuple-element.32) | copy-start | bytes 24580
  168.3 197.7 %copy-start.14 = (f32[2048]{0:T(1024)}, f32[2048]{0:T(1024)S(1)}, u32[]{:S(2)}) copy-start(f32[2048]{0:T(1024)S(1)} %fusion.74) | copy-start | bytes 24580
  321.1 23.1 %copy-start.5 = (bf16[2048,1024]{0,1:T(8,128)(2,1)S(1)}, bf16[2048,1024]{0,1:T(8,128)(2,1)}, u32[]{:S(2)}) copy-start(bf16[2048,1024]{0,1:T(8,128)(2,1)} %get-tuple-element.33) | copy-start | bytes 12582916
  344.2 21.7 %copy-start.17 = (f32[2048]{0:T(1024)S(1)}, f32[2048]{0:T(1024)}, u32[]{:S(2)}) copy-start(f32[2048]{0:T(1024)} %copy-done.16) | copy-start | bytes 24580
  344.2 21.7 %copy-start = (bf16[1,2048,1024]{1,2,0:T(8,128)(2,1)S(1)}, bf16[1,2048,1024]{1,2,0:T(8,128)(2,1)}, u32[]{:S(2)}) copy-start(bf16[1,2048,1024]{1,2,0:T(8,128)(2,1)} %copy.21) | copy-start | bytes 12582916
  370.9 2.0 copy-start.6
  392.5 153.1 %reduce-scatter.17.cloned.1.call-start = ((), (), s32[]{:S(2)}) async-start(), calls=%async_computation.11 | async-start | bytes 7667712 | tf_op jit(solution)/shard_map/reduce_scatter | solution.py:38
  420.2 21.1 %copy-start.19 = (f32[2048]{0:T(1024)S(1)}, f32[2048]{0:T(1024)}, u32[]{:S(2)}) copy-start(f32[2048]{0:T(1024)} %copy-done.18) | copy-start | bytes 24580
  420.2 125.5 %reduce-scatter.11.cloned.1.call-start = ((), (), s32[]{:S(2)}) async-start(), calls=%async_computation.8 | async-start | bytes 7667712 | tf_op jit(solution)/shard_map/reduce_scatter | solution.py:38
  466.9 0.7 copy-start.15
  466.9 112.3 %reduce-scatter.13.cloned.1.call-start = ((), (), s32[]{:S(2)}) async-start(), calls=%async_computation.9 | async-start | bytes 7667712 | tf_op jit(solution)/shard_map/reduce_scatter | solution.py:38
  492.9 133.4 %reduce-scatter.7.cloned.1.call-start = ((), (), s32[]{:S(2)}) async-start(), calls=%async_computation.6 | async-start | bytes 7667712 | tf_op jit(solution)/shard_map/reduce_scatter | solution.py:38
  524.2 149.1 %reduce-scatter.9.cloned.1.call-start = ((), (), s32[]{:S(2)}) async-start(), calls=%async_computation.7 | async-start | bytes 7667712 | tf_op jit(solution)/shard_map/reduce_scatter | solution.py:38
  545.5 243.4 %copy-start.2 = (bf16[2,416,1024]{2,1,0:T(8,128)(2,1)S(1)}, bf16[2,416,1024]{2,1,0:T(8,128)(2,1)}, u32[]{:S(2)}) copy-start(bf16[2,416,1024]{2,1,0:T(8,128)(2,1)} %param.15) | copy-start | bytes 5111812
  545.5 243.4 %all-reduce.3.cloned.1.call-start = ((), (), s32[]{:S(2)}) async-start(), calls=%async_computation.18 | async-start | bytes 10223616 | tf_op jit(solution)/shard_map/psum | solution.py:38
  789.0 7.6 copy-start.3
  789.0 7.6 copy-start.4
  789.0 8.0 copy-start.7
  789.0 9.4 %copy-start.8 = (f32[2,128,3328]{2,1,0:T(8,128)S(1)}, f32[2,128,3328]{2,1,0:T(8,128)}, u32[]{:S(2)}) copy-start(f32[2,128,3328]{2,1,0:T(8,128)} %param.16) | copy-start | bytes 10223620
  789.0 10.4 %copy-start.9 = (f32[2,128,3328]{2,1,0:T(8,128)S(1)}, f32[2,128,3328]{2,1,0:T(8,128)}, u32[]{:S(2)}) copy-start(f32[2,128,3328]{2,1,0:T(8,128)} %param.20) | copy-start | bytes 10223620
  789.0 10.5 %copy-start.10 = (bf16[1,128,3328]{2,1,0:T(8,128)(2,1)S(1)}, bf16[1,128,3328]{2,1,0:T(8,128)(2,1)}, u32[]{:S(2)}) copy-start(bf16[1,128,3328]{2,1,0:T(8,128)(2,1)} %get-tuple-element.9) | copy-start | bytes 2555908
  789.0 10.7 %copy-start.11 = (bf16[1,128,3328]{2,1,0:T(8,128)(2,1)S(1)}, bf16[1,128,3328]{2,1,0:T(8,128)(2,1)}, u32[]{:S(2)}) copy-start(bf16[1,128,3328]{2,1,0:T(8,128)(2,1)} %get-tuple-element.10) | copy-start | bytes 2555908
  789.0 11.0 %copy-start.12 = (bf16[1,128,3328]{2,1,0:T(8,128)(2,1)S(1)}, bf16[1,128,3328]{2,1,0:T(8,128)(2,1)}, u32[]{:S(2)}) copy-start(bf16[1,128,3328]{2,1,0:T(8,128)(2,1)} %get-tuple-element.11) | copy-start | bytes 2555908
  789.0 11.2 %copy-start.13 = (bf16[1,128,3328]{2,1,0:T(8,128)(2,1)S(1)}, bf16[1,128,3328]{2,1,0:T(8,128)(2,1)}, u32[]{:S(2)}) copy-start(bf16[1,128,3328]{2,1,0:T(8,128)(2,1)} %get-tuple-element.12) | copy-start | bytes 2555908
Sparse Core Ops, SparseCore 0:
  10.3 45.2 all-gather.12
  57.8 42.9 all-gather.14
  103.1 42.9 all-gather.16
  148.3 42.9 all-gather.22
  193.4 42.9 all-gather.20
  238.5 42.9 all-gather.18
  392.6 45.1 reduce-scatter.14
  440.2 44.6 reduce-scatter.16
  487.4 44.6 reduce-scatter.10
  534.4 44.6 reduce-scatter.12
  581.6 44.6 reduce-scatter.6
  628.6 44.6 reduce-scatter.8
  677.6 111.3 all-reduce.2
where the time goes:
time: 824 us; the launch traced here: 816 us
  matrix products  378 us (46%)
  waiting for transfers between devices  372 us (45%)
  local copies, waits for them, and re-layouts  26.2 us (3%)
  other arithmetic  24.8 us (3%)
  between operations  14.5 us (2%)
    dot_general x5, matrix products, layer(): gate = jnp.dot(a, w['w_gate'], preferred_element_type=jnp.float32)  137 us
    dot_general x5, matrix products, layer(): up = jnp.dot(a, w['w_up'], preferred_element_type=jnp.float32)  130 us
    reduce_scatter x6, waiting for transfers between devices, summed(): lax.psum_scatter(term, 's', scatter_dimension=0, tiled=True)  128 us
    all_gather x6, waiting for transfers between devices, fetched(): lax.all_gather(w[number], 's', axis=0, tiled=True)  127 us
    psum x1, waiting for transfers between devices, summed(): lax.psum(lax.psum_scatter(term, 's', scatter_dimension=0, tiled=True), 'r')  116 us
    dot_general x5, matrix products, matmul(): jnp.dot(a, w, preferred_element_type=jnp.float32).astype(jnp.bfloat16)  111 us
    unnamed x42, local copies, waits for them, and re-layouts  19.4 us
    convert_element_type x2, other arithmetic, adamw(): return ((w - 0.02 * step).astype(jnp.bfloat16), m, v)  16.8 us
  transfers between devices with their start and end apart: 13, of which 10 were waited for; matrix products, arithmetic and copies ran while one was open for 36% of the time, Pallas kernels for 0%

commit v1 on v0

v1 whole, which is shorter than its diff:
```python
import functools

import jax
import jax.numpy as jnp
from jax import lax
from jax.experimental import pallas as pl
from jax.experimental.pallas import tpu as pltpu
from jax.sharding import PartitionSpec as P

MESH = pl.DeviceIdType.MESH
f32, bf16 = jnp.float32, jnp.bfloat16
TN = 256
MC = 512
U = 128
VMEM_LIMIT = 62 * 2**20


def dot(a, b):
    return lax.dot_general(a, b, (((1,), (0,)), ((), ())), preferred_element_type=f32)


def dot_nt(a, b):
    return lax.dot_general(a, b, (((1,), (1,)), ((), ())), preferred_element_type=f32)


def normed(h):
    wide = h.astype(f32)
    scale = lax.rsqrt(jnp.mean(wide**2, -1, keepdims=True) + 1e-6)
    return (wide * scale).astype(bf16)


def chunks(n, step):
    return [pl.ds(i, step) for i in range(0, n, step)]


def forward_kernel(tiles, x_ref, wg_ref, wu_ref, wd_ref, s_ref, t_ref, p_ref, h_ref, a, acc):
    j = pl.program_id(0)
    tokens = x_ref.shape[0]

    @pl.when(j == 0)
    def _():
        for r in chunks(tokens, 256):
            a[r, :] = normed(x_ref[r, :])
            acc[r, :] = jnp.zeros_like(acc[r, :])

    for r in chunks(tokens, MC):
        g = dot(a[r, :], wg_ref[...])
        u = dot(a[r, :], wu_ref[...])
        sig = jax.nn.sigmoid(g)
        silu = g * sig
        s_ref[r, :] = silu
        t_ref[r, :] = u * (sig * (1 + g * (1 - sig)))
        p_ref[r, :] = (silu * u).astype(bf16)
    for r in chunks(tokens, MC):
        acc[r, :] += dot(p_ref[r, :], wd_ref[...])

    @pl.when(j == tiles - 1)
    def _():
        for r in chunks(tokens, 256):
            h_ref[r, :] = (x_ref[r, :].astype(f32) + acc[r, :].astype(bf16).astype(f32)).astype(bf16)


def forward(x, wg, wu, wd):
    tokens, d = x.shape
    ff = wg.shape[1]
    tiles = ff // TN
    whole = pl.BlockSpec((tokens, d), lambda j: (0, 0), pipeline_mode=pl.Buffered(1))
    cols = pl.BlockSpec((d, TN), lambda j: (0, j))
    hid = pl.BlockSpec((tokens, TN), lambda j: (0, j))
    return pl.pallas_call(
        functools.partial(forward_kernel, tiles),
        grid=(tiles,),
        in_specs=[whole, cols, cols, pl.BlockSpec((TN, d), lambda j: (j, 0))],
        out_specs=[hid, hid, hid, whole],
        out_shape=[jax.ShapeDtypeStruct((tokens, ff), f32)] * 2
        + [jax.ShapeDtypeStruct((tokens, ff), bf16), jax.ShapeDtypeStruct((tokens, d), bf16)],
        scratch_shapes=[pltpu.VMEM((tokens, d), bf16), pltpu.VMEM((tokens, d), f32)],
        compiler_params=pltpu.CompilerParams(vmem_limit_bytes=VMEM_LIMIT),
        cost_estimate=pl.CostEstimate(flops=6 * tokens * d * ff, bytes_accessed=10 * tokens * ff, transcendentals=0),
        name="forward0",
    )(x, wg, wu, wd)


def backward_kernel(tiles, x_ref, h_ref, dy_ref, wg_ref, wu_ref, wd1_ref, wd0_ref, s_ref, t_ref, p_ref,
                    ggu_ref, gwd_ref,
                    a, at, dy, accg, accu, pbuf, dg, du, dgu, dwd, r0gu, r0wd, s1, r1, s2, r2, s3, r3, fin,
                    lsem, s0s, s0r, s1s, s1r, s2s, s2r, s3s, s3r, ags, agr, ago):
    i = pl.program_id(0)
    tokens = a.shape[0]
    r, s = lax.axis_index("r"), lax.axis_index("s")
    y, z, xx, c = r // 4, r % 4, s // 2, s % 2
    total = 2 * tiles
    where = {"x": xx, "y": y, "z": z}
    ORDER = ("yzx", "zxy", "xyz")

    def to(dim, d):
        if dim == "y":
            return (0, lax.rem(y + d, 4) * 4 + z, s)
        if dim == "z":
            return (0, y * 4 + lax.rem(z + d, 4), s)
        return (0, r, lax.rem(xx + d, 4) * 2 + c)

    def remote(src, dst, ss, rs, dev):
        return pltpu.make_async_remote_copy(src_ref=src, dst_ref=dst, send_sem=ss, recv_sem=rs, device_id=dev, device_id_type=MESH)

    def stage0(tile):
        slot = lax.rem(tile, 2)
        peer = (0, r, s + 1 - 2 * c)
        return [
            remote(dgu.at[:, :, 1 - c], r0gu.at[slot], s0s.at[0], s0r.at[slot, 0], peer),
            remote(dwd.at[1 - c], r0wd.at[slot], s0s.at[1], s0r.at[slot, 1], peer),
        ]

    def exchange(n, src, dst, ss, rs, tile):
        slot = lax.rem(tile, 2)
        copies = []
        for q in range(3):
            dim = ORDER[q][n]
            for d in (1, 2, 3):
                copies.append(
                    remote(src.at[q, lax.rem(where[dim] + d, 4)], dst.at[slot, q, d - 1], ss.at[q, d - 1], rs.at[slot, q, d - 1], to(dim, d))
                )
        return copies

    stages = [functools.partial(exchange, n, *refs) for n, refs in enumerate(((s1, r1, s1s, s1r), (s2, r2, s2s, s2r), (s3, r3, s3s, s3r)))]

    def added(n, src, dst, tile, q):
        slot = lax.rem(tile, 2)
        own = src[q, where[ORDER[q][n]]].astype(f32)
        return (own + dst[slot, q, 0].astype(f32) + dst[slot, q, 1].astype(f32) + dst[slot, q, 2].astype(f32)).astype(bf16)

    def spread(tile, d):
        layer, j = 1 - tile // tiles, lax.rem(tile, tiles)
        to_r = lax.rem(r + d, 16)
        row = 16 * j + r
        owner = row // 26
        gu = (fin.at[tile, pl.ds(0, 2)], ggu_ref.at[layer, r, j])
        wd = (fin.at[tile, 2], gwd_ref.at[layer, row - 26 * owner, 4 * c + xx])
        return gu, wd, (0, to_r, s), (0, to_r, owner), owner

    def own_spread(tile, act):
        gu, wd, _, to_wd, owner = spread(tile, 0)
        if act == "start":
            pltpu.make_async_copy(*gu, agr.at[0]).start()

        @pl.when(owner == s)
        def _():
            if act == "start":
                pltpu.make_async_copy(*wd, agr.at[1]).start()

        @pl.when(owner != s)
        def _():
            cp = remote(*wd, ago.at[0], agr.at[1], to_wd)
            cp.start() if act == "start" else cp.wait_send()

    @pl.when(i == 0)
    def _():
        cp = [pltpu.make_async_copy(h_ref, a, lsem.at[0]), pltpu.make_async_copy(dy_ref, dy, lsem.at[1])]
        cp[0].start()
        cp[1].start()
        cp[0].wait()
        for rows in chunks(tokens, 256):
            v = normed(a[rows, :])
            a[rows, :] = v
            at[:, rows] = v.T
            accg[rows, :] = jnp.zeros_like(accg[rows, :])
            accu[rows, :] = jnp.zeros_like(accu[rows, :])
        cp[1].wait()

    @pl.when(i < tiles)
    def _():
        for rows in chunks(tokens, MC):
            g = dot(a[rows, :], wg_ref[...])
            u = dot(a[rows, :], wu_ref[...])
            d = dot_nt(dy[rows, :], wd1_ref[...]).astype(bf16).astype(f32)
            sig = jax.nn.sigmoid(g)
            silu = g * sig
            pbuf[rows, :] = (silu * u).astype(bf16)
            du[rows, :] = (d * silu).astype(bf16)
            dg[rows, :] = (d * u * (sig * (1 + g * (1 - sig)))).astype(bf16)
        for rows in chunks(tokens, MC):
            accg[rows, :] += dot_nt(dg[rows, :], wg_ref[...])
            accu[rows, :] += dot_nt(du[rows, :], wu_ref[...])

    @pl.when((i >= tiles) & (i < total))
    def _():
        for rows in chunks(tokens, MC):
            d = dot_nt(dy[rows, :], wd0_ref[...]).astype(bf16).astype(f32)
            du[rows, :] = (d * s_ref[rows, :]).astype(bf16)
            dg[rows, :] = (d * t_ref[rows, :]).astype(bf16)
            pbuf[rows, :] = p_ref[rows, :]

    @pl.when((i >= 4) & (i < total + 4))
    def _():
        tile = i - 4
        for cp in stages[2](tile):
            cp.wait()
        for q in range(3):
            fin[tile, q] = added(2, s3, r3, tile, q)
        own_spread(tile, "start")

        def send(d, _):
            gu, wd, to_gu, to_wd, _o = spread(tile, d)
            remote(*gu, ags.at[0], agr.at[0], to_gu).start()
            remote(*wd, ags.at[1], agr.at[1], to_wd).start()
            return 0

        lax.fori_loop(1, 16, send, 0)

    @pl.when((i >= 3) & (i < total + 3))
    def _():
        tile = i - 3
        for cp in stages[1](tile):
            cp.wait()
        for q in range(3):
            s3[q] = added(1, s2, r2, tile, q)
        for cp in stages[2](tile):
            cp.start()

    @pl.when((i >= 2) & (i < total + 2))
    def _():
        tile = i - 2
        for cp in stages[0](tile):
            cp.wait()
        for q in range(3):
            s2[q] = added(0, s1, r1, tile, q)
        for cp in stages[1](tile):
            cp.start()

    @pl.when((i >= 1) & (i < total + 1))
    def _():
        tile = i - 1
        slot = lax.rem(tile, 2)
        for cp in stage0(tile):
            cp.wait()
        for xi in range(4):
            for k in range(8):
                for h in range(2):
                    rows, cols = pl.ds(16 * k, 16), pl.ds(U * h, U)
                    yi, zi = k // 2, 2 * (k % 2) + h
                    for q, at_ in ((0, (yi, zi, xi)), (1, (zi, xi, yi))):
                        v = dgu[q, xi, c, rows, cols].astype(f32) + r0gu[slot, q, xi, rows, cols].astype(f32)
                        s1[(q, *at_)] = v.astype(bf16)
                    unit = 2 * k + h
                    rows, cols = pl.ds(16 * unit, 16), pl.ds(U * xi, U)
                    v = dwd[c, rows, cols].astype(f32) + r0wd[slot, rows, cols].astype(f32)
                    s1[2, xi, unit // 4, unit % 4] = v.astype(bf16)
        for cp in stages[0](tile):
            cp.start()

    @pl.when(i < total)
    def _():
        for q, one in ((0, dg), (1, du)):
            g = dot(at[...], one[...]).astype(bf16)
            dgu[q] = g.reshape(dgu.shape[1:])
        g = dot(pbuf[...].T, dy[...]).astype(bf16)
        dwd[0] = g[:, :512]
        dwd[1] = g[:, 512:]
        for cp in stage0(i):
            cp.start()

    @pl.when(i == tiles - 1)
    def _():
        cp = pltpu.make_async_copy(h_ref, a, lsem.at[0])
        cp.start()
        cp.wait()
        for rows in chunks(tokens, 256):
            da = (accg[rows, :].astype(bf16).astype(f32) + accu[rows, :].astype(bf16).astype(f32)).astype(bf16).astype(f32)
            wide = a[rows, :].astype(f32)
            scale = lax.rsqrt(jnp.mean(wide**2, -1, keepdims=True) + 1e-6)
            along = jnp.sum(da * wide, -1, keepdims=True)
            by_h = da * scale - wide * (along * (scale * scale * scale) * (1.0 / wide.shape[-1]))
            dy[rows, :] = (dy[rows, :].astype(f32) + by_h.astype(bf16).astype(f32)).astype(bf16)
        cp = pltpu.make_async_copy(x_ref, a, lsem.at[0])
        cp.start()
        cp.wait()
        for rows in chunks(tokens, 256):
            at[:, rows] = normed(a[rows, :]).T

    @pl.when(i == total + 3)
    def _():
        remote(ggu_ref.at[:, pl.ds(0, 15)], ggu_ref.at[:, pl.ds(0, 15)], ags.at[0], agr.at[0], to("y", 1)).wait_send()
        half = ggu_ref.at[0, pl.ds(0, 15)]
        remote(half, half, ags.at[1], agr.at[1], to("y", 1)).wait_send()

        def done(tile, _):
            own_spread(tile, "wait")
            return 0

        lax.fori_loop(0, total, done, 0)
        pltpu.make_async_copy(ggu_ref, ggu_ref, agr.at[0]).wait()
        pltpu.make_async_copy(gwd_ref, gwd_ref, agr.at[1]).wait()


def backward(x, h, dy, wg, wu, wd1, wd0, s, t, p):
    tokens, d = x.shape
    ff = wg.shape[1]
    tiles = ff // TN
    last = tiles - 1
    anywhere = pl.BlockSpec(memory_space=pl.ANY)
    cols = pl.BlockSpec((d, TN), lambda i: (0, jnp.minimum(i, last)))
    clamp = lambda i: jnp.clip(i - tiles, 0, last)
    hid = pl.BlockSpec((tokens, TN), lambda i: (0, clamp(i)))
    dma = pltpu.SemaphoreType.DMA
    unit = (16, U)
    return pl.pallas_call(
        functools.partial(backward_kernel, tiles),
        grid=(2 * tiles + 4,),
        in_specs=[anywhere] * 3
        + [cols, cols, pl.BlockSpec((TN, d), lambda i: (jnp.minimum(i, last), 0)), pl.BlockSpec((TN, d), lambda i: (clamp(i), 0))]
        + [hid] * 3,
        out_specs=[anywhere] * 2,
        out_shape=[jax.ShapeDtypeStruct((2, 16, tiles, 2, *unit), bf16), jax.ShapeDtypeStruct((2, 26, 8, *unit), bf16)],
        scratch_shapes=[
            pltpu.VMEM((tokens, d), bf16),
            pltpu.VMEM((d, tokens), bf16),
            pltpu.VMEM((tokens, d), bf16),
            pltpu.VMEM((tokens, d), f32),
            pltpu.VMEM((tokens, d), f32),
            pltpu.VMEM((tokens, TN), bf16),
            pltpu.VMEM((tokens, TN), bf16),
            pltpu.VMEM((tokens, TN), bf16),
            pltpu.VMEM((2, 4, 2, 128, TN), bf16),
            pltpu.VMEM((2, TN, 512), bf16),
            pltpu.VMEM((2, 2, 4, 128, TN), bf16),
            pltpu.VMEM((2, TN, 512), bf16),
            pltpu.VMEM((3, 4, 4, 4, *unit), bf16),
            pltpu.VMEM((2, 3, 3, 4, 4, *unit), bf16),
            pltpu.VMEM((3, 4, 4, *unit), bf16),
            pltpu.VMEM((2, 3, 3, 4, *unit), bf16),
            pltpu.VMEM((3, 4, *unit), bf16),
            pltpu.VMEM((2, 3, 3, *unit), bf16),
            pltpu.VMEM((2 * tiles, 3, *unit), bf16),
            dma((2,)),
            dma((2,)),
            dma((2, 2)),
        ]
        + [dma((3, 3)), dma((2, 3, 3))] * 3
        + [dma((2,)), dma((2,)), dma((1,))],
        compiler_params=pltpu.CompilerParams(vmem_limit_bytes=VMEM_LIMIT, has_side_effects=True),
        cost_estimate=pl.CostEstimate(flops=24 * tokens * d * ff, bytes_accessed=10 * tokens * ff, transcendentals=0),
        name="backward",
    )(x, h, dy, wg, wu, wd1, wd0, s, t, p)


def adamw(w, m, v, g):
    m = 0.9 * m + 0.1 * g
    v = 0.95 * v + 0.05 * g * g
    step = m * lax.rsqrt(v + 1e-8) + 0.1 * w
    return (w - 0.02 * step).astype(bf16), m, v


def update_kernel(ggu_ref, gwd_ref, *refs):
    ins, outs = refs[:9], refs[9:]
    for q in range(2):
        for k in range(8):
            for h in range(2):
                at_ = (0, pl.ds(16 * k, 16), pl.ds(U * h, U))
                new = adamw(ins[q][at_].astype(f32), ins[3 + q][at_], ins[6 + q][at_], ggu_ref[0, 2 * k + h, 0, q].astype(f32))
                for n, one in enumerate(new):
                    outs[3 * n + q][at_] = one
    for k in range(2):
        for h in range(8):
            at_ = (0, pl.ds(16 * k, 16), pl.ds(U * h, U))
            new = adamw(ins[2][at_].astype(f32), ins[5][at_], ins[8][at_], gwd_ref[0, k, h].astype(f32))
            for n, one in enumerate(new):
                outs[3 * n + 2][at_] = one


def update(ggu, gwd, weights, m, v):
    layers, rows, ff = weights[0].shape
    tiles = ff // TN
    gu = pl.BlockSpec((1, rows, TN), lambda n, j: (n, 0, j))
    wd = pl.BlockSpec((1, 32, weights[2].shape[2]), lambda n, j: (n, j, 0))
    specs = [gu, gu, wd] * 3
    arrays = (*weights, *m, *v)
    return pl.pallas_call(
        update_kernel,
        grid=(layers, tiles),
        in_specs=[
            pl.BlockSpec((1, 16, 1, 2, 16, U), lambda n, j: (n, 0, j, 0, 0, 0)),
            pl.BlockSpec((1, 2, 8, 16, U), lambda n, j: (n, j, 0, 0, 0)),
        ]
        + specs,
        out_specs=specs,
        out_shape=[jax.ShapeDtypeStruct(one.shape, one.dtype) for one in arrays],
        compiler_params=pltpu.CompilerParams(vmem_limit_bytes=48 * 2**20),
        name="update",
    )(ggu, gwd, *arrays)


def solution(mesh):
    def fetched(w, number):
        return lax.all_gather(w[number], "s", axis=0, tiled=True)

    def step(x, dy, *arrays):
        weights, m, v = (arrays[i : i + 3] for i in (0, 3, 6))
        w0 = [fetched(w, 0) for w in weights]
        w1 = [fetched(w, 1) for w in weights]
        s, t, p, h = forward(x[0], *w0)
        ggu, gwd = backward(x[0], h, dy[0], *w1, w0[2], s, t, p)
        return tuple(update(ggu, gwd, weights, m, v))

    states, cut = P(("rep", "r", "s"), None, None), P(None, "s", None)
    return jax.shard_map(
        step,
        mesh=mesh,
        in_specs=(states, states) + (cut,) * 9,
        out_specs=(P("rep", "s", None),) * 9,
        check_vma=False,
    )
```

time: 824 us -> 615 us (0.75)
  matrix products: 378 us -> 0 us
  Pallas kernels: 0 us -> 377 us
  waiting for transfers between devices: 372 us -> 212 us
  other arithmetic: 24.8 us -> 0 us
  local copies, waits for them, and re-layouts: 26.2 us -> 8.96 us
    dot_general x15 -> x0, matrix products: 378 us -> none  [the longest x5 137 us: layer(): gate = jnp.dot(a, w['w_gate'], preferred_element_type=jnp.float32)]
    pallas_call x0 -> x3, Pallas kernels: none -> 377 us  [the longest x1 294 us: backward(): pl.pallas_call(functools.partial(backward_kernel, tiles), grid=(2 * tiles...]
    reduce_scatter x6 -> x0, waiting for transfers between devices: 128 us -> none  [summed(): lax.psum_scatter(term, 's', scatter_dimension=0, tiled=True)]
    psum x1 -> x0, waiting for transfers between devices: 116 us -> none  [summed(): lax.psum(lax.psum_scatter(term, 's', scatter_dimension=0, tiled=True), 'r')]
    all_gather x6, waiting for transfers between devices: 127 us -> 211 us  [fetched(): return lax.all_gather(w[number], 's', axis=0, tiled=True)]
    convert_element_type x2 -> x0, other arithmetic: 16.8 us -> none  [adamw(): return ((w - 0.02 * step).astype(jnp.bfloat16), m, v)]
    unnamed x42 -> x10, local copies, waits for them, and re-layouts: 19.4 us -> 3.53 us
  transfers between devices with their start and end apart: 13 -> 6, of which waited for: 10 -> 5; matrix products, arithmetic and copies ran while one was open for 36% -> 0% of each run, Pallas kernels for 0% -> 9%
where the time goes in v1:
time: 615 us; the launch traced here: 613 us
  Pallas kernels  377 us (61%)
  waiting for transfers between devices  212 us (34%)
  between operations  14.2 us (2%)
  local copies, waits for them, and re-layouts  8.96 us (1%)
    pallas_call x1, Pallas kernels, backward(): pl.pallas_call(functools.partial(backward_kernel, tiles), grid=(2 * tiles...  294 us
    all_gather x6, waiting for transfers between devices, fetched(): return lax.all_gather(w[number], 's', axis=0, tiled=True)  211 us
    pallas_call x1, Pallas kernels, forward(): pl.pallas_call(functools.partial(forward_kernel, tiles), grid=(tiles,), i...  55.7 us
    pallas_call x1, Pallas kernels, update(): pl.pallas_call(update_kernel, grid=(layers, tiles), in_specs=[pl.BlockSpe...  27.9 us
  transfers between devices with their start and end apart: 6, of which 5 were waited for; matrix products, arithmetic and copies ran while one was open for 0% of the time, Pallas kernels for 9%

profile of v1, /device:TPU:0, one launch (start us, length us, event | category | flops | bytes accessed | tf_op | source)
XLA Modules:
  0.0 612.9 jit_solution(6446323272062563489)
XLA Ops:
  7.2 0.0 copy-start
  7.2 0.0 all-gather.17.cloned.1.call-start
  7.2 2.8 fusion
  10.1 0.0 copy-start.2
  10.1 0.0 all-gather.17.cloned.1.call-update
  10.1 0.0 all-gather.13.cloned.1.call-start
  10.2 0.0 copy-done
  10.2 1.3 fusion.2
  11.5 0.0 all-gather.13.cloned.1.call-update
  11.5 0.0 all-gather.15.cloned.1.call-start
  11.5 0.6 copy-done.2
  12.1 1.3 fusion.1
  13.4 0.0 all-gather.15.cloned.1.call-update
  13.5 0.0 all-gather.19.cloned.1.call-start
  13.5 0.5 all-gather.19.cloned.1.call-update
  14.0 0.0 all-gather.21.cloned.1.call-start
  14.1 0.5 all-gather.21.cloned.1.call-update
  14.6 0.0 all-gather.23.cloned.1.call-start
  14.7 0.5 all-gather.23.cloned.1.call-update
  15.2 40.4 %all-gather.17.cloned.1.call-done = bf16[1,3328,1024]{2,1,0:T(8,128)(2,1)} async-done(((bf16[1,416,1024]{2,1,0:T(8,128)(2,1)}), bf16[1,3328,1024]{2,1,0:T(8,128)(2,1)}) %all-gather.17.cloned.1.call-update) | async-done | bytes 6815760 | tf_op jit(solution)/shard_map/all_gather | solution.py:394
  55.6 45.3 %all-gather.13.cloned.1.call-done = bf16[1,1024,3328]{2,1,0:T(8,128)(2,1)} async-done(((bf16[1,128,3328]{2,1,0:T(8,128)(2,1)}), bf16[1,1024,3328]{2,1,0:T(8,128)(2,1)}) %all-gather.13.cloned.1.call-update) | async-done | bytes 6815760 | tf_op jit(solution)/shard_map/all_gather | solution.py:394
  100.9 45.3 %all-gather.15.cloned.1.call-done = bf16[1,1024,3328]{2,1,0:T(8,128)(2,1)} async-done(((bf16[1,128,3328]{2,1,0:T(8,128)(2,1)}), bf16[1,1024,3328]{2,1,0:T(8,128)(2,1)}) %all-gather.15.cloned.1.call-update) | async-done | bytes 6815760 | tf_op jit(solution)/shard_map/all_gather | solution.py:394
  146.1 55.7 %forward0.1 = (f32[2048,3328]{1,0:T(8,128)}, f32[2048,3328]{1,0:T(8,128)}, bf16[2048,3328]{1,0:T(8,128)(2,1)}, bf16[2048,1024]{1,0:T(8,128)(2,1)}) custom-call(bf16[2048,1024]{1,0:T(8,128)(2,1)} %bitcast.15, bf16[1024,3328]{1,0:T(8,128)(2,1)} %bitcast.10, bf16[1024,3328]{1,0:T(8,128)(2,1)} %bitcast.12, bf16[3328,1024]{1,0:T(8,128)(2,1)} %bitcast.8), custom_call_target="tpu_custom_call" | custom-call | flops 41875931136 | bytes 68157440 | tf_op jit(solution)/shard_map/forward0/pallas_call | solution.py:70
  201.8 0.0 all-gather.19.cloned.1.call-done
  201.9 34.5 %all-gather.21.cloned.1.call-done = bf16[1,1024,3328]{2,1,0:T(8,128)(2,1)} async-done(((bf16[1,128,3328]{2,1,0:T(8,128)(2,1)}), bf16[1,1024,3328]{2,1,0:T(8,128)(2,1)}) %all-gather.21.cloned.1.call-update) | async-done | bytes 6815760 | tf_op jit(solution)/shard_map/all_gather | solution.py:394
  236.4 45.1 %all-gather.23.cloned.1.call-done = bf16[1,3328,1024]{2,1,0:T(8,128)(2,1)} async-done(((bf16[1,416,1024]{2,1,0:T(8,128)(2,1)}), bf16[1,3328,1024]{2,1,0:T(8,128)(2,1)}) %all-gather.23.cloned.1.call-update) | async-done | bytes 6815760 | tf_op jit(solution)/shard_map/all_gather | solution.py:394
  281.5 0.0 copy-start.1
  281.6 293.7 %backward.1 = (bf16[2,16,13,2,16,128]{5,4,3,2,1,0:T(8,128)(2,1)}, bf16[2,26,8,16,128]{4,3,2,1,0:T(8,128)(2,1)}) custom-call(bf16[2048,1024]{1,0:T(8,128)(2,1)} %bitcast.16, bf16[2048,1024]{1,0:T(8,128)(2,1)} %get-tuple-element.15.h_ref, bf16[2048,1024]{1,0:T(8,128)(2,1)} %bitcast.17, bf16[1024,3328]{1,0:T(8,128)(2,1)} %bitcast.11, ...), custom_call_target="tpu_custom_call" | custom-call | flops 167503724544 | bytes 68157440 | tf_op jit(solution)/shard_map/backward/pallas_call | solution.py:306
  575.2 0.0 copy-done.1
  575.2 0.0 copy-start.3
  575.2 1.4 copy-done.3
  576.7 0.0 copy-start.4
  576.7 1.5 copy-done.4
  578.1 27.9 %update.1 = (bf16[2,128,3328]{2,1,0:T(8,128)(2,1)}, bf16[2,128,3328]{2,1,0:T(8,128)(2,1)}, bf16[2,416,1024]{2,1,0:T(8,128)(2,1)}, f32[2,128,3328]{2,1,0:T(8,128)...) custom-call(bf16[2,16,13,2,16,128]{5,4,3,2,1,0:T(8,128)(2,1)} %get-t, ...), custom_call_target="tpu_custom_call" | custom-call | tf_op jit(solution)/shard_map/update/pallas_call | solution.py:377
Async XLA Ops:
  7.2 3.0 copy-start
  7.2 48.4 %all-gather.17.cloned.1.call-start = ((), (), s32[]{:S(2)}) async-start(), calls=%async_computation.2 | async-start | bytes 7667712 | tf_op jit(solution)/shard_map/all_gather | solution.py:394
  10.1 2.1 copy-start.2
  10.1 90.8 %all-gather.13.cloned.1.call-start = ((), (), s32[]{:S(2)}) async-start(), calls=%async_computation | async-start | bytes 7667712 | tf_op jit(solution)/shard_map/all_gather | solution.py:394
  11.5 134.7 %all-gather.15.cloned.1.call-start = ((), (), s32[]{:S(2)}) async-start(), calls=%async_computation.1 | async-start | bytes 7667712 | tf_op jit(solution)/shard_map/all_gather | solution.py:394
  13.5 188.4 %all-gather.19.cloned.1.call-start = ((), (), s32[]{:S(2)}) async-start(), calls=%async_computation.3 | async-start | bytes 7667712 | tf_op jit(solution)/shard_map/all_gather | solution.py:394
  14.0 222.4 %all-gather.21.cloned.1.call-start = ((), (), s32[]{:S(2)}) async-start(), calls=%async_computation.4 | async-start | bytes 7667712 | tf_op jit(solution)/shard_map/all_gather | solution.py:394
  14.6 266.9 %all-gather.23.cloned.1.call-start = ((), (), s32[]{:S(2)}) async-start(), calls=%async_computation.5 | async-start | bytes 7667712 | tf_op jit(solution)/shard_map/all_gather | solution.py:394
  281.5 293.7 %copy-start.1 = (bf16[2,128,3328]{2,1,0:T(8,128)(2,1)S(1)}, bf16[2,128,3328]{2,1,0:T(8,128)(2,1)}, u32[]{:S(2)}) copy-start(bf16[2,128,3328]{2,1,0:T(8,128)(2,1)} %refs_0_.1) | copy-start | bytes 5111812
  575.2 1.5 copy-start.3
  576.7 1.5 copy-start.4
Sparse Core Ops, SparseCore 0:
  10.3 45.2 all-gather.16
  57.8 42.9 all-gather.12
  103.1 42.9 all-gather.14
  148.3 42.9 all-gather.18
  193.4 42.9 all-gather.20
  238.5 42.9 all-gather.22

commit v2 on v1

--- a/solution.py
+++ b/solution.py
@@ -33,49 +33,202 @@
     return [pl.ds(i, step) for i in range(0, n, step)]
 
 
-def forward_kernel(tiles, x_ref, wg_ref, wu_ref, wd_ref, s_ref, t_ref, p_ref, h_ref, a, acc):
-    j = pl.program_id(0)
+def forward_kernel(tiles, x_ref, wg_in, wu_in, wd_in, s_ref, t_ref, p_ref, h_ref, wg_all, wu_all, wd_all,
+                   a, acc, p_all, tg, tu, td, osem, orecv, lsem, asend, bsend, dsend, arecv, brecv, drecv):
+    k = pl.program_id(0)
     tokens = x_ref.shape[0]
-
-    @pl.when(j == 0)
-    def _():
-        for r in chunks(tokens, 256):
-            a[r, :] = normed(x_ref[r, :])
-            acc[r, :] = jnp.zeros_like(acc[r, :])
-
-    for r in chunks(tokens, MC):
-        g = dot(a[r, :], wg_ref[...])
-        u = dot(a[r, :], wu_ref[...])
-        sig = jax.nn.sigmoid(g)
-        silu = g * sig
-        s_ref[r, :] = silu
-        t_ref[r, :] = u * (sig * (1 + g * (1 - sig)))
-        p_ref[r, :] = (silu * u).astype(bf16)
-    for r in chunks(tokens, MC):
-        acc[r, :] += dot(p_ref[r, :], wd_ref[...])
-
-    @pl.when(j == tiles - 1)
-    def _():
-        for r in chunks(tokens, 256):
-            h_ref[r, :] = (x_ref[r, :].astype(f32) + acc[r, :].astype(bf16).astype(f32)).astype(bf16)
+    r, s = lax.axis_index("r"), lax.axis_index("s")
+    y, z, x, c = r // 4, r % 4, s // 2, s % 2
+    items = 2 * tiles
+
+    def remote(src, dst, ss, rs, dev):
+        return pltpu.make_async_remote_copy(src_ref=src, dst_ref=dst, send_sem=ss, recv_sem=rs, device_id=dev, device_id_type=MESH)
+
+    peer = (0, r, s + 1 - 2 * c)
+
+    def own_copies():
+        blocks = (
+            (wg_in, wg_all.at[:, pl.ds(128 * s, 128), :]),
+            (wu_in, wu_all.at[:, pl.ds(128 * s, 128), :]),
+            (wd_in, wd_all.at[:, pl.ds(416 * s, 416), :]),
+        )
+        here = [pltpu.make_async_copy(src, dst, lsem.at[0, n]) for n, (src, dst) in enumerate(blocks)]
+        there = [remote(src, dst, osem.at[n], orecv.at[n], peer) for n, (src, dst) in enumerate(blocks)]
+        return here + there
+
+    def parts(item, sx):
+        layer, j = item // tiles, lax.rem(item, tiles)
+        cols = pl.ds(pl.multiple_of(TN * j, TN), TN)
+        owner = 2 * sx + c
+        down = pl.ds(32 * j, 32), pl.ds(416 * owner + 32 * j, 32)
+        return layer, (
+            (wg_in, pl.ds(32 * y, 32), cols, wg_all, pl.ds(128 * owner + 32 * y, 32), "y"),
+            (wu_in, pl.ds(32 * z, 32), cols, wu_all, pl.ds(128 * owner + 32 * z, 32), "z"),
+            (wd_in, down[0], pl.ds(pl.multiple_of(128 * y, 128), 128), wd_all, down[1], "y"),
+            (wd_in, down[0], pl.ds(pl.multiple_of(512 + 128 * z, 128), 128), wd_all, down[1], "z"),
+        )
+
+    def along(dim, d):
+        if dim == "y":
+            return (0, lax.rem(y + d, 4) * 4 + z, s)
+        return (0, y * 4 + lax.rem(z + d, 4), s)
+
+    def bytes_of(rows, sems, item, recv):
+        some = wg_all.at[0, pl.ds(0, rows), pl.ds(0, 768)]
+        if recv:
+            pltpu.make_async_copy(some, some, sems.at[item]).wait()
+        else:
+            pltpu.make_async_copy(some, some, sems.at[0]).wait()
+
+    @pl.when(k == 0)
+    def _():
+        for cp in own_copies():
+            cp.start()
+
+    @pl.when(k < items)
+    def _():
+        layer, some = parts(k, x)
+        for d in (1, 2, 3):
+            for src, rows, cols, dst, there, _dim in some:
+                to = (0, r, 2 * lax.rem(x + d, 4) + c)
+                remote(src.at[layer, rows, cols], dst.at[layer, there, cols], asend.at[0], arecv.at[k], to).start()
+
+    @pl.when((k >= 2) & (k < items + 2))
+    def _():
+        item = k - 2
+        bytes_of(96, arecv, item, True)
+        for e in (1, 2, 3):
+            layer, some = parts(item, lax.rem(x + e, 4))
+            for _src, _rows, cols, dst, there, dim in some:
+                ref = dst.at[layer, there, cols]
+                for d in (1, 2, 3):
+                    remote(ref, ref, bsend.at[0], brecv.at[item], along(dim, d)).start()
+
+    @pl.when((k >= 4) & (k < items + 4))
+    def _():
+        item = k - 4
+        bytes_of(288, brecv, item, True)
+        layer, j = item // tiles, lax.rem(item, tiles)
+        cols = pl.ds(pl.multiple_of(TN * j, TN), TN)
+        for e in (1, 2, 3):
+            owner = 2 * lax.rem(x + e, 4) + c
+            for dst in (wg_all, wu_all):
+                ref = dst.at[layer, pl.ds(128 * owner, 128), cols]
+                remote(ref, ref, dsend.at[0], drecv.at[item], peer).start()
+            ref = wd_all.at[layer, pl.ds(416 * owner + 32 * j, 32), :]
+            remote(ref, ref, dsend.at[0], drecv.at[item], peer).start()
+
+    @pl.when(k == 5)
+    def _():
+        for cp in own_copies():
+            cp.wait()
+
+    @pl.when(k == 0)
+    def _():
+        for rows in chunks(tokens, 256):
+            a[rows, :] = normed(x_ref[rows, :])
+            acc[rows, :] = jnp.zeros_like(acc[rows, :])
+
+    def loads(tile):
+        slot = lax.rem(tile, 2)
+        cols = pl.ds(pl.multiple_of(TN * tile, TN), TN)
+        return [
+            pltpu.make_async_copy(wg_all.at[0, :, cols], tg.at[slot], lsem.at[1 + slot, 0]),
+            pltpu.make_async_copy(wu_all.at[0, :, cols], tu.at[slot], lsem.at[1 + slot, 1]),
+        ]
+
+    def load_down(tile):
+        slot = lax.rem(tile, 2)
+        return pltpu.make_async_copy(wd_all.at[0, pl.ds(TN * tile, TN), :], td.at[slot], lsem.at[1 + slot, 2])
+
+    @pl.when((k >= 5) & (k < items + 5))
+    def _():
+        bytes_of(384, drecv, k - 5, True)
+
+    @pl.when((k >= 5) & (k < tiles + 5))
+    def _():
+        for cp in loads(k - 5):
+            cp.start()
+
+    @pl.when((k >= tiles + 5) & (k < items + 5))
+    def _():
+        load_down(k - tiles - 5).start()
+
+    @pl.when((k >= 6) & (k < tiles + 6))
+    def _():
+        tile = k - 6
+        slot = lax.rem(tile, 2)
+        for cp in loads(tile):
+            cp.wait()
+        for rows in chunks(tokens, MC):
+            g = dot(a[rows, :], tg[slot])
+            u = dot(a[rows, :], tu[slot])
+            sig = jax.nn.sigmoid(g)
+            silu = g * sig
+            s_ref[rows, :] = silu
+            t_ref[rows, :] = u * (sig * (1 + g * (1 - sig)))
+            p = (silu * u).astype(bf16)
+            p_ref[rows, :] = p
+            p_all[tile, rows, :] = p
+
+    @pl.when((k >= tiles + 6) & (k < items + 6))
+    def _():
+        tile = k - tiles - 6
+        load_down(tile).wait()
+        for rows in chunks(tokens, MC):
+            acc[rows, :] += dot(p_all[tile, rows, :], td[lax.rem(tile, 2)])
+
+    @pl.when(k == items + 5)
+    def _():
+        for rows in chunks(tokens, 256):
+            h_ref[rows, :] = (x_ref[rows, :].astype(f32) + acc[rows, :].astype(bf16).astype(f32)).astype(bf16)
+
+        def sent(item, _):
+            bytes_of(96, asend, item, False)
+            bytes_of(288, bsend, item, False)
+            bytes_of(384, dsend, item, False)
+            return 0
+
+        lax.fori_loop(0, items, sent, 0)
 
 
 def forward(x, wg, wu, wd):
     tokens, d = x.shape
-    ff = wg.shape[1]
+    ff = wg.shape[2]
     tiles = ff // TN
-    whole = pl.BlockSpec((tokens, d), lambda j: (0, 0), pipeline_mode=pl.Buffered(1))
-    cols = pl.BlockSpec((d, TN), lambda j: (0, j))
-    hid = pl.BlockSpec((tokens, TN), lambda j: (0, j))
+    one = pl.Buffered(1)
+    anywhere = pl.BlockSpec(memory_space=pl.ANY)
+    whole = pl.BlockSpec((tokens, d), lambda k: (0, 0), pipeline_mode=one)
+    hid = pl.BlockSpec((tokens, TN), lambda k: (0, jnp.clip(k - 6, 0, tiles - 1)))
+    ours = [pl.BlockSpec(w.shape, lambda k: (0, 0, 0), pipeline_mode=one) for w in (wg, wu, wd)]
+    dma = pltpu.SemaphoreType.DMA
     return pl.pallas_call(
         functools.partial(forward_kernel, tiles),
-        grid=(tiles,),
-        in_specs=[whole, cols, cols, pl.BlockSpec((TN, d), lambda j: (j, 0))],
-        out_specs=[hid, hid, hid, whole],
+        grid=(2 * tiles + 6,),
+        in_specs=[whole, *ours],
+        out_specs=[hid, hid, hid, whole, anywhere, anywhere, anywhere],
         out_shape=[jax.ShapeDtypeStruct((tokens, ff), f32)] * 2
-        + [jax.ShapeDtypeStruct((tokens, ff), bf16), jax.ShapeDtypeStruct((tokens, d), bf16)],
-        scratch_shapes=[pltpu.VMEM((tokens, d), bf16), pltpu.VMEM((tokens, d), f32)],
-        compiler_params=pltpu.CompilerParams(vmem_limit_bytes=VMEM_LIMIT),
+        + [jax.ShapeDtypeStruct((tokens, ff), bf16), jax.ShapeDtypeStruct((tokens, d), bf16)]
+        + [jax.ShapeDtypeStruct((2, d, ff), bf16)] * 2
+        + [jax.ShapeDtypeStruct((2, ff, d), bf16)],
+        scratch_shapes=[
+            pltpu.VMEM((tokens, d), bf16),
+            pltpu.VMEM((tokens, d), f32),
+            pltpu.VMEM((tiles, tokens, TN), bf16),
+            pltpu.VMEM((2, d, TN), bf16),
+            pltpu.VMEM((2, d, TN), bf16),
+            pltpu.VMEM((2, TN, d), bf16),
+            dma((3,)),
+            dma((3,)),
+            dma((3, 3)),
+            dma((1,)),
+            dma((1,)),
+            dma((1,)),
+            dma((2 * tiles,)),
+            dma((2 * tiles,)),
+            dma((2 * tiles,)),
+        ],
+        compiler_params=pltpu.CompilerParams(vmem_limit_bytes=VMEM_LIMIT, has_side_effects=True),
         cost_estimate=pl.CostEstimate(flops=6 * tokens * d * ff, bytes_accessed=10 * tokens * ff, transcendentals=0),
         name="forward0",
     )(x, wg, wu, wd)
@@ -292,13 +445,13 @@
         pltpu.make_async_copy(gwd_ref, gwd_ref, agr.at[1]).wait()
 
 
-def backward(x, h, dy, wg, wu, wd1, wd0, s, t, p):
+def backward(x, h, dy, wg, wu, wd, s, t, p):
     tokens, d = x.shape
-    ff = wg.shape[1]
+    ff = wg.shape[2]
     tiles = ff // TN
     last = tiles - 1
     anywhere = pl.BlockSpec(memory_space=pl.ANY)
-    cols = pl.BlockSpec((d, TN), lambda i: (0, jnp.minimum(i, last)))
+    cols = pl.BlockSpec((None, d, TN), lambda i: (1, 0, jnp.minimum(i, last)))
     clamp = lambda i: jnp.clip(i - tiles, 0, last)
     hid = pl.BlockSpec((tokens, TN), lambda i: (0, clamp(i)))
     dma = pltpu.SemaphoreType.DMA
@@ -307,7 +460,7 @@
         functools.partial(backward_kernel, tiles),
         grid=(2 * tiles + 4,),
         in_specs=[anywhere] * 3
-        + [cols, cols, pl.BlockSpec((TN, d), lambda i: (jnp.minimum(i, last), 0)), pl.BlockSpec((TN, d), lambda i: (clamp(i), 0))]
+        + [cols, cols, pl.BlockSpec((None, TN, d), lambda i: (1, jnp.minimum(i, last), 0)), pl.BlockSpec((None, TN, d), lambda i: (0, clamp(i), 0))]
         + [hid] * 3,
         out_specs=[anywhere] * 2,
         out_shape=[jax.ShapeDtypeStruct((2, 16, tiles, 2, *unit), bf16), jax.ShapeDtypeStruct((2, 26, 8, *unit), bf16)],
@@ -340,7 +493,7 @@
         compiler_params=pltpu.CompilerParams(vmem_limit_bytes=VMEM_LIMIT, has_side_effects=True),
         cost_estimate=pl.CostEstimate(flops=24 * tokens * d * ff, bytes_accessed=10 * tokens * ff, transcendentals=0),
         name="backward",
-    )(x, h, dy, wg, wu, wd1, wd0, s, t, p)
+    )(x, h, dy, wg, wu, wd, wd, s, t, p)
 
 
 def adamw(w, m, v, g):
@@ -390,15 +543,10 @@
 
 
 def solution(mesh):
-    def fetched(w, number):
-        return lax.all_gather(w[number], "s", axis=0, tiled=True)
-
     def step(x, dy, *arrays):
         weights, m, v = (arrays[i : i + 3] for i in (0, 3, 6))
-        w0 = [fetched(w, 0) for w in weights]
-        w1 = [fetched(w, 1) for w in weights]
-        s, t, p, h = forward(x[0], *w0)
-        ggu, gwd = backward(x[0], h, dy[0], *w1, w0[2], s, t, p)
+        s, t, p, h, *whole = forward(x[0], *weights)
+        ggu, gwd = backward(x[0], h, dy[0], *whole, s, t, p)
         return tuple(update(ggu, gwd, weights, m, v))
 
     states, cut = P(("rep", "r", "s"), None, None), P(None, "s", None)

time: 615 us -> 444 us (0.72)
  waiting for transfers between devices: 212 us -> 0 us
  Pallas kernels: 377 us -> 438 us
  between operations: 14.2 us -> 0.84 us
    all_gather x6 -> x0, waiting for transfers between devices: 211 us -> none  [fetched(): return lax.all_gather(w[number], 's', axis=0, tiled=True)]
    pallas_call x1, Pallas kernels: 55.7 us -> 116 us  [forward(): pl.pallas_call(functools.partial(forward_kernel, tiles), grid=(2 * tiles...]
  transfers between devices with their start and end apart: 6 -> 0, of which waited for: 5 -> 0; matrix products, arithmetic and copies ran while one was open for 0% -> 0% of each run, Pallas kernels for 9% -> 0%
where the time goes in v2:
time: 444 us; the launch traced here: 442 us
  Pallas kernels  438 us (99%)
    pallas_call x1, Pallas kernels, backward(): pl.pallas_call(functools.partial(backward_kernel, tiles), grid=(2 * tiles...  294 us
    pallas_call x1, Pallas kernels, forward(): pl.pallas_call(functools.partial(forward_kernel, tiles), grid=(2 * tiles...  116 us
    pallas_call x1, Pallas kernels, update(): pl.pallas_call(update_kernel, grid=(layers, tiles), in_specs=[pl.BlockSpe...  27.9 us

profile of v2, /device:TPU:0, one launch (start us, length us, event | category | flops | bytes accessed | tf_op | source)
XLA Modules:
  0.0 442.0 jit_solution(8263853047919294096)
XLA Ops:
  0.6 116.2 %forward0.1 = (f32[2048,3328]{1,0:T(8,128)}, f32[2048,3328]{1,0:T(8,128)}, bf16[2048,3328]{1,0:T(8,128)(2,1)}, bf16[2048,1024]{1,0:T(8,128)(2,1)}, bf16[2,1024,3...) custom-call(bf16[2048,1024]{1,0:T(8,128)(2,1)} %bitcast.2, ...), custom_call_target="tpu_custom_call" | custom-call | flops 41875931136 | bytes 68157440 | tf_op jit(solution)/shard_map/forward0/pallas_call | solution.py:205
  116.8 0.0 copy-start
  116.9 294.2 %backward.1 = (bf16[2,16,13,2,16,128]{5,4,3,2,1,0:T(8,128)(2,1)}, bf16[2,26,8,16,128]{4,3,2,1,0:T(8,128)(2,1)}) custom-call(bf16[2048,1024]{1,0:T(8,128)(2,1)} %bitcast.3, bf16[2048,1024]{1,0:T(8,128)(2,1)} %get-tuple-element.18.h_ref, bf16[2048,1024]{1,0:T(8,128)(2,1)} %bitcast.4, bf16[2,1024,3328]{2,1,0:T(8,128)(2,1)} %get-tuple-element.19.wg_ref, ...), custom_call_target="tpu_custom_call" | custom-call | flops 167503724544 | bytes 68157440 | tf_op jit(solution)/shard_map/backward/pallas_call | solution.py:459
  411.0 0.0 copy-done
  411.0 0.0 copy-start.1
  411.1 1.4 copy-done.1
  412.5 0.0 copy-start.2
  412.5 1.5 copy-done.2
  414.0 27.9 %update.1 = (bf16[2,128,3328]{2,1,0:T(8,128)(2,1)}, bf16[2,128,3328]{2,1,0:T(8,128)(2,1)}, bf16[2,416,1024]{2,1,0:T(8,128)(2,1)}, f32[2,128,3328]{2,1,0:T(8,128)...) custom-call(bf16[2,16,13,2,16,128]{5,4,3,2,1,0:T(8,128)(2,1)} %get-t, ...), custom_call_target="tpu_custom_call" | custom-call | tf_op jit(solution)/shard_map/update/pallas_call | solution.py:530
Async XLA Ops:
  116.8 294.2 %copy-start = (bf16[2,128,3328]{2,1,0:T(8,128)(2,1)S(1)}, bf16[2,128,3328]{2,1,0:T(8,128)(2,1)}, u32[]{:S(2)}) copy-start(bf16[2,128,3328]{2,1,0:T(8,128)(2,1)} %refs_0_.1) | copy-start | bytes 5111812
  411.0 1.5 copy-start.1
  412.5 1.5 copy-start.2

commit v3 on v0

v3 whole, which is shorter than its diff:
```python
import functools

import jax
import jax.numpy as jnp
from jax import lax
from jax.experimental import pallas as pl
from jax.experimental.pallas import tpu as pltpu
from jax.sharding import PartitionSpec as P

MESH = pl.DeviceIdType.MESH
f32, bf16 = jnp.float32, jnp.bfloat16
TN = 256
MC = 512
U = 128
VMEM_LIMIT = 67043328


def dot(a, b):
    return lax.dot_general(a, b, (((1,), (0,)), ((), ())), preferred_element_type=f32)


def dot_nt(a, b):
    return lax.dot_general(a, b, (((1,), (1,)), ((), ())), preferred_element_type=f32)


def normed(h):
    wide = h.astype(f32)
    scale = lax.rsqrt(jnp.mean(wide**2, -1, keepdims=True) + 1e-6)
    return (wide * scale).astype(bf16)


def chunks(n, step):
    return [pl.ds(i, step) for i in range(0, n, step)]


class Place:
    def __init__(self):
        self.r, self.s = lax.axis_index("r"), lax.axis_index("s")
        self.y, self.z, self.x, self.c = self.r // 4, self.r % 4, self.s // 2, self.s % 2
        self.peer = (0, self.r, self.s + 1 - 2 * self.c)

    def along(self, dim, d):
        if dim == "y":
            return (0, lax.rem(self.y + d, 4) * 4 + self.z, self.s)
        if dim == "z":
            return (0, self.y * 4 + lax.rem(self.z + d, 4), self.s)
        return (0, self.r, lax.rem(self.x + d, 4) * 2 + self.c)


def remote(src, dst, ss, rs, dev):
    return pltpu.make_async_remote_copy(src_ref=src, dst_ref=dst, send_sem=ss, recv_sem=rs, device_id=dev, device_id_type=MESH)


class Fetch:
    A, B, D = 288, 864, 1152

    def __init__(self, place, own, whole, some, sends, recvs):
        self.p, self.own, self.whole, self.some, self.sends, self.recvs = place, own, whole, some, sends, recvs

    def quarters(self, refs, owner):
        p, (wg, wu, wd) = self.p, refs
        base, low = (0, 0) if owner is None else (128 * owner, 32 * owner)
        rows = pl.ds(low, 32)
        return (
            (wg.at[pl.ds(base + 32 * p.y, 32), :], "y"),
            (wu.at[pl.ds(base + 32 * p.z, 32), :], "z"),
            (wd.at[rows, pl.ds(pl.multiple_of(128 * p.y, 128), 128)], "y"),
            (wd.at[rows, pl.ds(pl.multiple_of(512 + 128 * p.z, 128), 128)], "z"),
        )

    def wait(self, rows, sem):
        some = self.some.at[pl.ds(0, 1), pl.ds(0, rows)] if rows <= 1024 else self.some.at[pl.ds(0, 2), pl.ds(0, rows // 2)]
        pltpu.make_async_copy(some, some, sem).wait()

    def a(self, tile, n):
        src, dst = self.quarters(self.own(tile), None), self.quarters(self.whole(tile), self.p.s)
        for d in (1, 2, 3):
            for (one, _), (other, _) in zip(src, dst, strict=True):
                remote(one, other, self.sends.at[0], self.recvs[0].at[n], self.p.along("x", d)).start()

    def b(self, tile, n):
        self.wait(self.A, self.recvs[0].at[n])
        for e in (1, 2, 3):
            for ref, dim in self.quarters(self.whole(tile), 2 * lax.rem(self.p.x + e, 4) + self.p.c):
                for d in (1, 2, 3):
                    remote(ref, ref, self.sends.at[1], self.recvs[1].at[n], self.p.along(dim, d)).start()

    def d(self, tile, n):
        self.wait(self.B, self.recvs[1].at[n])
        wg, wu, wd = self.whole(tile)
        for e in (1, 2, 3):
            owner = 2 * lax.rem(self.p.x + e, 4) + self.p.c
            for ref in (wg.at[pl.ds(128 * owner, 128), :], wu.at[pl.ds(128 * owner, 128), :], wd.at[pl.ds(32 * owner, 32), :]):
                remote(ref, ref, self.sends.at[2], self.recvs[2].at[n], self.p.peer).start()

    def here(self, n):
        self.wait(self.D, self.recvs[2].at[n])

    def sent(self, count):
        def one(_n, _):
            for k, rows in enumerate((self.A, self.B, self.D)):
                self.wait(rows, self.sends.at[k])
            return 0

        lax.fori_loop(0, count, one, 0)


def forward_kernel(tiles, early, x_ref, wg_in, wu_in, wd_in, s_ref, t_ref, p_ref, h_ref, wg_all, wu_all, wd_all,
                   a, acc, wgp, wup, tg, tu, td, osem, orecv, lsem, sends, arecv, brecv, drecv):
    k = pl.program_id(0)
    tokens = x_ref.shape[0]
    place = Place()
    fetch = [
        Fetch(
            place,
            lambda j, n=n: (wgp.at[n, j], wup.at[n, j], wd_in.at[n, j]),
            lambda j, n=n: (wg_all.at[n, j], wu_all.at[n, j], wd_all.at[n, j]),
            wg_all.at[0],
            sends,
            (arecv, brecv, drecv),
        )
        for n in range(2)
    ]

    def own_copies(n):
        blocks = (
            (wgp.at[n], wg_all.at[n, :, pl.ds(128 * place.s, 128), :]),
            (wup.at[n], wu_all.at[n, :, pl.ds(128 * place.s, 128), :]),
            (wd_in.at[n], wd_all.at[n, :, pl.ds(32 * place.s, 32), :]),
        )
        here = [pltpu.make_async_copy(src, dst, lsem.at[n, m]) for m, (src, dst) in enumerate(blocks)]
        there = [remote(src, dst, osem.at[n, m], orecv.at[n, m], place.peer) for m, (src, dst) in enumerate(blocks)]
        return here + there

    def permute(n):
        def rows_of(i, _):
            rows = pl.ds(pl.multiple_of(16 * i, 16), 16)
            for src, dst in ((wg_in, wgp), (wu_in, wup)):
                v = src[n, rows, :]
                for j in range(tiles):
                    for h in range(2):
                        parts = [v[:, 416 * o + 32 * j : 416 * o + 32 * j + 32] for o in range(4 * h, 4 * h + 4)]
                        dst[n, j, rows, U * h : U * h + U] = jnp.concatenate(parts, axis=1)
            return 0

        lax.fori_loop(0, 8, rows_of, 0)

    for n in range(2):

        @pl.when(k == n)
        def _(n=n):
            permute(n)
            for cp in own_copies(n):
                cp.start()

    @pl.when(k < tiles)
    def _():
        fetch[0].a(k, k)

    m = k // 2 - 2
    even = lax.rem(k, 2) == 0

    @pl.when(even & (m >= 0) & (m < early))
    def _():
        fetch[1].a(m, tiles + m)

    @pl.when((k >= 2) & (k < tiles + 2))
    def _():
        fetch[0].b(k - 2, k - 2)

    @pl.when(even & (m >= 1) & (m < early + 1))
    def _():
        fetch[1].b(m - 1, tiles + m - 1)

    @pl.when((k >= 4) & (k < tiles + 4))
    def _():
        fetch[0].d(k - 4, k - 4)

    @pl.when(even & (m >= 2) & (m < early + 2))
    def _():
        fetch[1].d(m - 2, tiles + m - 2)

    @pl.when(k == 0)
    def _():
        for rows in chunks(tokens, 256):
            a[rows, :] = normed(x_ref[rows, :])
            acc[rows, :] = jnp.zeros_like(acc[rows, :])

    for n in range(2):

        @pl.when(k == 4 + n)
        def _(n=n):
            for cp in own_copies(n):
                cp.wait()

    def loads(tile):
        slot = lax.rem(tile, 2)
        pairs = ((wg_all.at[0, tile], tg), (wu_all.at[0, tile], tu), (wd_all.at[0, tile], td))
        return [pltpu.make_async_copy(src, dst.at[slot], lsem.at[2 + slot, q]) for q, (src, dst) in enumerate(pairs)]

    @pl.when((k >= 5) & (k < tiles + 5))
    def _():
        fetch[0].here(k - 5)
        for cp in loads(k - 5):
            cp.start()

    @pl.when(k >= 6)
    def _():
        tile = k - 6
        slot = lax.rem(tile, 2)
        for cp in loads(tile):
            cp.wait()
        for rows in chunks(tokens, MC):
            g = dot(a[rows, :], tg[slot])
            u = dot(a[rows, :], tu[slot])
            sig = jax.nn.sigmoid(g)
            silu = g * sig
            s_ref[rows, :] = silu
            t_ref[rows, :] = u * (sig * (1 + g * (1 - sig)))
            p_ref[rows, :] = (silu * u).astype(bf16)
        for rows in chunks(tokens, MC):
            acc[rows, :] += dot(p_ref[rows, :], td[slot])

    @pl.when(k == tiles + 5)
    def _():
        for rows in chunks(tokens, 256):
            h_ref[rows, :] = (x_ref[rows, :].astype(f32) + acc[rows, :].astype(bf16).astype(f32)).astype(bf16)
        for n in range(early):
            fetch[1].here(tiles + n)
        fetch[0].sent(tiles + early)


def forward(x, wg, wu, wd, early):
    tokens, d = x.shape
    ff = wg.shape[2]
    tiles = ff // TN
    one = pl.Buffered(1)
    anywhere = pl.BlockSpec(memory_space=pl.ANY)
    whole = pl.BlockSpec((tokens, d), lambda k: (0, 0), pipeline_mode=one)
    hid = pl.BlockSpec((tokens, TN), lambda k: (0, jnp.clip(k - 6, 0, tiles - 1)))
    wd = wd.reshape(2, tiles, 32, d)
    ours = [pl.BlockSpec(w.shape, lambda k, n=w.ndim: (0,) * n, pipeline_mode=one) for w in (wg, wu, wd)]
    dma = pltpu.SemaphoreType.DMA
    return pl.pallas_call(
        functools.partial(forward_kernel, tiles, early),
        grid=(tiles + 6,),
        in_specs=[whole, *ours],
        out_specs=[hid, hid, hid, whole, anywhere, anywhere, anywhere],
        out_shape=[jax.ShapeDtypeStruct((tokens, ff), f32)] * 2
        + [jax.ShapeDtypeStruct((tokens, ff), bf16), jax.ShapeDtypeStruct((tokens, d), bf16)]
        + [jax.ShapeDtypeStruct((2, tiles, d, TN), bf16)] * 2
        + [jax.ShapeDtypeStruct((2, tiles, TN, d), bf16)],
        scratch_shapes=[
            pltpu.VMEM((tokens, d), bf16),
            pltpu.VMEM((tokens, d), f32),
            pltpu.VMEM((2, tiles, 128, TN), bf16),
            pltpu.VMEM((2, tiles, 128, TN), bf16),
            pltpu.VMEM((2, d, TN), bf16),
            pltpu.VMEM((2, d, TN), bf16),
            pltpu.VMEM((2, TN, d), bf16),
            dma((2, 3)),
            dma((2, 3)),
            dma((4, 3)),
            dma((3,)),
            dma((tiles + early,)),
            dma((tiles + early,)),
            dma((tiles + early,)),
        ],
        compiler_params=pltpu.CompilerParams(vmem_limit_bytes=VMEM_LIMIT, has_side_effects=True),
        cost_estimate=pl.CostEstimate(flops=6 * tokens * d * ff, bytes_accessed=10 * tokens * ff, transcendentals=0),
        name="forward0",
    )(x, wg, wu, wd)


def backward_kernel(tiles, early, x_ref, h_ref, dy_ref, wg_ref, wu_ref, wd_ref, wd0_ref, s_ref, t_ref, p_ref,
                    sums_ref, wg_more, wu_more, wd_more,
                    a, at, dy, accg, accu, pbuf, dg, du, tg, tu, td, dgu, dwd, r0gu, r0wd, s1, r1, s2, r2, s3, r3, fin,
                    lsem, tsem, s0s, s0r, s1s, s1r, s2s, s2r, s3s, s3r, ags, agr, sends, arecv, brecv, drecv):
    i = pl.program_id(0)
    tokens = a.shape[0]
    place = Place()
    r, c = place.r, place.c
    total = 2 * tiles
    where = {"x": place.x, "y": place.y, "z": place.z}
    ORDER = ("yzx", "zxy", "xyz")

    def stage0(tile):
        slot = lax.rem(tile, 2)
        return [
            remote(dgu.at[slot, :, :, 1 - c], r0gu.at[slot], s0s.at[slot, 0], s0r.at[slot, 0], place.peer),
            remote(dwd.at[slot, :, 1 - c], r0wd.at[slot], s0s.at[slot, 1], s0r.at[slot, 1], place.peer),
        ]

    STAGES = ((s1, r1, s1s, s1r, 2, 4), (s2, r2, s2s, s2r, 1, 2), (s3, r3, s3s, s3r, 1, 2))

    def exchange(n, tile):
        src, dst, ss, rs, held, slots = STAGES[n]
        own, slot = lax.rem(tile, held), lax.rem(tile, slots)
        for q in range(3):
            dim = ORDER[q][n]
            for d in (1, 2, 3):
                part = src.at[own, q, lax.rem(where[dim] + d, 4)]
                remote(part, dst.at[slot, q, d - 1], ss.at[own], rs.at[slot], place.along(dim, d)).start()

    def arrived(n, tile):
        src, dst, ss, rs, held, slots = STAGES[n]
        own, slot = lax.rem(tile, held), lax.rem(tile, slots)
        sent = src.at[own, :, pl.ds(0, 3)]
        pltpu.make_async_copy(sent, sent, ss.at[own]).wait()
        pltpu.make_async_copy(dst.at[slot], dst.at[slot], rs.at[slot]).wait()

    def added(n, tile, q):
        src, dst, _ss, _rs, held, slots = STAGES[n]
        slot = lax.rem(tile, slots)
        own = src[lax.rem(tile, held), q, where[ORDER[q][n]]].astype(f32)
        return (own + dst[slot, q, 0].astype(f32) + dst[slot, q, 1].astype(f32) + dst[slot, q, 2].astype(f32)).astype(bf16)

    def spread(tile):
        src, dst = fin.at[tile], sums_ref.at[1 - tile // tiles, r, lax.rem(tile, tiles)]
        pltpu.make_async_copy(src, dst, agr.at[0]).start()

        def one(d, _):
            remote(src, dst, ags.at[0], agr.at[0], (0, lax.rem(r + d, 16), place.s)).start()
            return 0

        lax.fori_loop(1, 16, one, 0)

    fetch = Fetch(
        place,
        lambda j: (wg_ref.at[1, j, pl.ds(128 * place.s, 128), :], wu_ref.at[1, j, pl.ds(128 * place.s, 128), :], wd_ref.at[1, j, pl.ds(32 * place.s, 32), :]),
        lambda j: (wg_more.at[j - early], wu_more.at[j - early], wd_more.at[j - early]),
        wg_more,
        sends,
        (arecv, brecv, drecv),
    )

    def load(tile, act):
        slot = lax.rem(tile, 2)
        arrays = ((wg_ref, wg_more, tg, 256), (wu_ref, wu_more, tu, 256), (wd_ref, wd_more, td, 64))

        @pl.when(tile < early)
        def _():
            for q, (first, _more, dst, _n) in enumerate(arrays):
                act(pltpu.make_async_copy(first.at[1, tile], dst.at[slot], tsem.at[slot, q]))

        @pl.when(tile >= early)
        def _():
            for q, (first, more, dst, n) in enumerate(arrays):
                for e in range(4):
                    rows = pl.ds(n * lax.rem(place.x + e, 4), n)
                    src = first.at[1, tile, rows, :] if e == 0 else more.at[tile - early, rows, :]
                    cp = pltpu.make_async_copy(src, dst.at[slot, rows, :], tsem.at[slot, q])
                    act(cp)

    @pl.when(i == 0)
    def _():
        cp = [pltpu.make_async_copy(h_ref, a, lsem.at[0]), pltpu.make_async_copy(dy_ref, dy, lsem.at[1])]
        cp[0].start()
        cp[1].start()
        load(i, lambda cp: cp.start())
        cp[0].wait()
        for rows in chunks(tokens, 256):
            v = normed(a[rows, :])
            a[rows, :] = v
            at[:, rows] = v.T
            accg[rows, :] = jnp.zeros_like(accg[rows, :])
            accu[rows, :] = jnp.zeros_like(accu[rows, :])
        cp[1].wait()

    @pl.when((i >= early - 1) & (i < tiles - 1))
    def _():
        fetch.here(i + 1 - early)

    @pl.when(i < tiles - 1)
    def _():
        load(i + 1, lambda cp: cp.start())

    def by_weights(p):
        slot = lax.rem(i, 2)
        for q, one in ((0, dg), (1, du)):
            dgu[slot, q] = dot(at[...], one[...]).astype(bf16).reshape(dgu.shape[2:])
        dwd[slot] = dot(p[...].T, dy[...]).astype(bf16).reshape(dwd.shape[1:])

    @pl.when(i < tiles)
    def _():
        slot = lax.rem(i, 2)
        load(i, lambda cp: cp.wait())
        for rows in chunks(tokens, MC):
            g = dot(a[rows, :], tg[slot])
            u = dot(a[rows, :], tu[slot])
            d = dot_nt(dy[rows, :], td[slot]).astype(bf16).astype(f32)
            sig = jax.nn.sigmoid(g)
            silu = g * sig
            pbuf[rows, :] = (silu * u).astype(bf16)
            du[rows, :] = (d * silu).astype(bf16)
            dg[rows, :] = (d * u * (sig * (1 + g * (1 - sig)))).astype(bf16)
        for rows in chunks(tokens, MC):
            accg[rows, :] += dot_nt(dg[rows, :], tg[slot])
            accu[rows, :] += dot_nt(du[rows, :], tu[slot])
        by_weights(pbuf)

    @pl.when((i >= tiles) & (i < total))
    def _():
        for rows in chunks(tokens, MC):
            d = dot_nt(dy[rows, :], wd0_ref[...]).astype(bf16).astype(f32)
            du[rows, :] = (d * s_ref[rows, :]).astype(bf16)
            dg[rows, :] = (d * t_ref[rows, :]).astype(bf16)
        by_weights(p_ref)

    @pl.when(i == tiles - 1)
    def _():
        pltpu.make_async_copy(h_ref, a, lsem.at[0]).start()

    @pl.when((i >= 5) & (i < total + 5))
    def _():
        tile = i - 5
        arrived(2, tile)
        for q in range(3):
            fin[tile, q] = added(2, tile, q)

    @pl.when((i >= 4) & (i < total + 4))
    def _():
        tile = i - 4
        arrived(1, tile)
        for q in range(3):
            s3[0, q] = added(1, tile, q)
        exchange(2, tile)

    @pl.when((i >= 3) & (i < total + 3))
    def _():
        tile = i - 3
        arrived(0, tile)
        for q in range(3):
            s2[0, q] = added(0, tile, q)
        exchange(1, tile)

    @pl.when((i >= 1) & (i < total + 1))
    def _():
        tile = i - 1
        slot = lax.rem(tile, 2)
        for cp in stage0(tile):
            cp.wait()
        for xi in range(4):
            for k in range(8):
                for h in range(2):
                    rows, cols = pl.ds(16 * k, 16), pl.ds(U * h, U)
                    yi, zi = k // 2, 2 * (k % 2) + h
                    for q, at_ in ((0, (yi, zi, xi)), (1, (zi, xi, yi))):
                        v = dgu[slot, q, xi, c, rows, cols].astype(f32) + r0gu[slot, q, xi, rows, cols].astype(f32)
                        s1[(slot, q, *at_)] = v.astype(bf16)
                    rows, cols = pl.ds(16 * (yi // 2), 16), pl.ds(U * (4 * (yi % 2) + zi), U)
                    v = dwd[slot, xi, c, rows, cols].astype(f32) + r0wd[slot, xi, rows, cols].astype(f32)
                    s1[slot, 2, xi, yi, zi] = v.astype(bf16)
        exchange(0, tile)

    @pl.when(i < total)
    def _():
        for cp in stage0(i):
            cp.start()

    for stage, lag in ((fetch.d, 3), (fetch.b, 4), (fetch.a, 5)):

        @pl.when((i + lag >= early) & (i + lag < tiles))
        def _(stage=stage, lag=lag):
            stage(i + lag, i + lag - early)

    @pl.when((i >= 5) & (i < total + 5))
    def _():
        spread(i - 5)

    @pl.when(i == tiles - 1)
    def _():
        pltpu.make_async_copy(h_ref, a, lsem.at[0]).wait()
        parts = chunks(tokens, 256)
        for n, rows in enumerate(parts):
            da = (accg[rows, :].astype(bf16).astype(f32) + accu[rows, :].astype(bf16).astype(f32)).astype(bf16).astype(f32)
            wide = a[rows, :].astype(f32)
            scale = lax.rsqrt(jnp.mean(wide**2, -1, keepdims=True) + 1e-6)
            along = jnp.sum(da * wide, -1, keepdims=True)
            by_h = da * scale - wide * (along * (scale * scale * scale) * (1.0 / wide.shape[-1]))
            dy[rows, :] = (dy[rows, :].astype(f32) + by_h.astype(bf16).astype(f32)).astype(bf16)
            pltpu.make_async_copy(x_ref.at[rows, :], a.at[rows, :], lsem.at[n]).start()
        for n, rows in enumerate(parts):
            pltpu.make_async_copy(x_ref.at[rows, :], a.at[rows, :], lsem.at[n]).wait()
            at[:, rows] = normed(a[rows, :]).T

    @pl.when(i == total + 4)
    def _():
        fetch.sent(tiles - early)
        some = sums_ref.at[:, pl.ds(0, 15)]
        pltpu.make_async_copy(some, some, ags.at[0]).wait()
        pltpu.make_async_copy(sums_ref, sums_ref, agr.at[0]).wait()


def backward(x, h, dy, wg, wu, wd, s, t, p, early):
    tokens, d = x.shape
    ff = s.shape[1]
    tiles = ff // TN
    last = tiles - 1
    anywhere = pl.BlockSpec(memory_space=pl.ANY)
    clamp = lambda i: jnp.clip(i - tiles, 0, last)
    hid = pl.BlockSpec((tokens, TN), lambda i: (0, clamp(i)))
    dma = pltpu.SemaphoreType.DMA
    unit = (16, U)
    return pl.pallas_call(
        functools.partial(backward_kernel, tiles, early),
        grid=(2 * tiles + 5,),
        in_specs=[anywhere] * 6 + [pl.BlockSpec((None, None, TN, d), lambda i: (0, clamp(i), 0, 0))] + [hid] * 3,
        out_specs=[anywhere] * 4,
        out_shape=[
            jax.ShapeDtypeStruct((2, 16, tiles, 3, *unit), bf16),
            jax.ShapeDtypeStruct((tiles - early, d, TN), bf16),
            jax.ShapeDtypeStruct((tiles - early, d, TN), bf16),
            jax.ShapeDtypeStruct((tiles - early, TN, d), bf16),
        ],
        scratch_shapes=[
            pltpu.VMEM((tokens, d), bf16),
            pltpu.VMEM((d, tokens), bf16),
            pltpu.VMEM((tokens, d), bf16),
            pltpu.VMEM((tokens, d), f32),
            pltpu.VMEM((tokens, d), f32),
            pltpu.VMEM((tokens, TN), bf16),
            pltpu.VMEM((tokens, TN), bf16),
            pltpu.VMEM((tokens, TN), bf16),
            pltpu.VMEM((2, d, TN), bf16),
            pltpu.VMEM((2, d, TN), bf16),
            pltpu.VMEM((2, TN, d), bf16),
            pltpu.VMEM((2, 2, 4, 2, 128, TN), bf16),
            pltpu.VMEM((2, 4, 2, 32, d), bf16),
            pltpu.VMEM((2, 2, 4, 128, TN), bf16),
            pltpu.VMEM((2, 4, 32, d), bf16),
            pltpu.VMEM((2, 3, 4, 4, 4, *unit), bf16),
            pltpu.VMEM((4, 3, 3, 4, 4, *unit), bf16),
            pltpu.VMEM((1, 3, 4, 4, *unit), bf16),
            pltpu.VMEM((2, 3, 3, 4, *unit), bf16),
            pltpu.VMEM((1, 3, 4, *unit), bf16),
            pltpu.VMEM((2, 3, 3, *unit), bf16),
            pltpu.VMEM((2 * tiles, 3, *unit), bf16),
            dma((8,)),
            dma((2, 3)),
            dma((2, 2)),
            dma((2, 2)),
            dma((2,)),
            dma((4,)),
            dma((1,)),
            dma((2,)),
            dma((1,)),
            dma((2,)),
            dma((1,)),
            dma((1,)),
            dma((3,)),
            dma((tiles - early,)),
            dma((tiles - early,)),
            dma((tiles - early,)),
        ],
        compiler_params=pltpu.CompilerParams(vmem_limit_bytes=VMEM_LIMIT, has_side_effects=True),
        cost_estimate=pl.CostEstimate(flops=24 * tokens * d * ff, bytes_accessed=10 * tokens * ff, transcendentals=0),
        name="backward",
    )(x, h, dy, wg, wu, wd, wd, s, t, p)[0]


def adamw(w, m, v, g):
    m = 0.9 * m + 0.1 * g
    v = 0.95 * v + 0.05 * g * g
    step = m * lax.rsqrt(v + 1e-8) + 0.1 * w
    return (w - 0.02 * step).astype(bf16), m, v


def update_kernel(tiles, sgu_ref, sd_ref, *refs):
    ins, outs = refs[:9], refs[9:]
    i = pl.program_id(0)

    def one(q, at_, g):
        new = adamw(ins[q][at_].astype(f32), ins[3 + q][at_], ins[6 + q][at_], g.astype(f32))
        for n, value in enumerate(new):
            outs[3 * n + q][at_] = value

    @pl.when(i < 16)
    def _():
        for q in range(2):
            for n in range(2 * tiles):
                parts = []
                for k in range(4 * n, 4 * n + 4):
                    owner, j = k // tiles, k % tiles
                    parts.append(sgu_ref[0, owner // 4, j, q, :, 32 * (owner % 4) : 32 * (owner % 4) + 32])
                one(q, (0, slice(None), pl.ds(U * n, U)), jnp.concatenate(parts, axis=1))

    @pl.when(i >= 16)
    def _():
        def tile(j, _):
            for k in range(2):
                for h in range(8):
                    at_ = (0, pl.ds(pl.multiple_of(32 * j + 16 * k, 16), 16), pl.ds(U * h, U))
                    one(2, at_, sd_ref[0, 8 * k + h, j, 0])
            return 0

        lax.fori_loop(0, tiles, tile, 0)


def update(sums, weights, m, v):
    _layers, rows, ff = weights[0].shape
    tiles = ff // TN
    gu = pl.BlockSpec((1, 16, ff), lambda i: (jnp.minimum(i, 15) // 8, jnp.minimum(i, 15) % 8, 0))
    down = lambda i: jnp.maximum(i - 16, 0)
    wd = pl.BlockSpec((1, *weights[2].shape[1:]), lambda i: (down(i), 0, 0))
    specs = [gu, gu, wd] * 3
    arrays = (*weights, *m, *v)
    return pl.pallas_call(
        functools.partial(update_kernel, tiles),
        grid=(18,),
        in_specs=[
            pl.BlockSpec((1, 2, tiles, 3, 16, U), lambda i: (jnp.minimum(i, 15) // 8, jnp.minimum(i, 15) % 8, 0, 0, 0, 0)),
            pl.BlockSpec((1, 16, tiles, 1, 16, U), lambda i: (down(i), 0, 0, 2, 0, 0)),
        ]
        + specs,
        out_specs=specs,
        out_shape=[jax.ShapeDtypeStruct(one.shape, one.dtype) for one in arrays],
        compiler_params=pltpu.CompilerParams(vmem_limit_bytes=VMEM_LIMIT),
        name="update",
    )(sums, sums, *arrays)


def solution(mesh):
    def step(x, dy, *arrays):
        weights, m, v = (arrays[i : i + 3] for i in (0, 3, 6))
        early = 5
        s, t, p, h, *whole = forward(x[0], *weights, early)
        sums = backward(x[0], h, dy[0], *whole, s, t, p, early)
        return tuple(update(sums, weights, m, v))

    states, cut = P(("rep", "r", "s"), None, None), P(None, "s", None)
    return jax.shard_map(
        step,
        mesh=mesh,
        in_specs=(states, states) + (cut,) * 9,
        out_specs=(P("rep", "s", None),) * 9,
        check_vma=False,
    )
```

time: 824 us -> 397 us (0.48)
  Pallas kernels: 0 us -> 395 us
  matrix products: 378 us -> 0 us
  waiting for transfers between devices: 372 us -> 0 us
  local copies, waits for them, and re-layouts: 26.2 us -> 0 us
  other arithmetic: 24.8 us -> 0 us
  between operations: 14.5 us -> 0.81 us
    pallas_call x0 -> x3, Pallas kernels: none -> 395 us  [the longest x1 267 us: backward(): pl.pallas_call(functools.partial(backward_kernel, tiles, early), grid=(2...]
    dot_general x15 -> x0, matrix products: 378 us -> none  [the longest x5 137 us: layer(): gate = jnp.dot(a, w['w_gate'], preferred_element_type=jnp.float32)]
    reduce_scatter x6 -> x0, waiting for transfers between devices: 128 us -> none  [summed(): lax.psum_scatter(term, 's', scatter_dimension=0, tiled=True)]
    all_gather x6 -> x0, waiting for transfers between devices: 127 us -> none  [fetched(): lax.all_gather(w[number], 's', axis=0, tiled=True)]
    psum x1 -> x0, waiting for transfers between devices: 116 us -> none  [summed(): lax.psum(lax.psum_scatter(term, 's', scatter_dimension=0, tiled=True), 'r')]
    unnamed x42 -> x0, local copies, waits for them, and re-layouts: 19.4 us -> none
    convert_element_type x2 -> x0, other arithmetic: 16.8 us -> none  [adamw(): return ((w - 0.02 * step).astype(jnp.bfloat16), m, v)]
  transfers between devices with their start and end apart: 13 -> 0, of which waited for: 10 -> 0; matrix products, arithmetic and copies ran while one was open for 36% -> 0% of each run, Pallas kernels for 0% -> 0%
where the time goes in v3:
time: 397 us; the launch traced here: 396 us
  Pallas kernels  395 us (99%)
    pallas_call x1, Pallas kernels, backward(): pl.pallas_call(functools.partial(backward_kernel, tiles, early), grid=(2...  267 us
    pallas_call x1, Pallas kernels, forward(): pl.pallas_call(functools.partial(forward_kernel, tiles, early), grid=(til...  99.6 us
    pallas_call x1, Pallas kernels, update(): pl.pallas_call(functools.partial(update_kernel, tiles), grid=(18,), in_sp...  28.3 us

profile of v3, /device:TPU:0, one launch (start us, length us, event | category | flops | bytes accessed | tf_op | source)
XLA Modules:
  0.0 396.1 jit_solution(9529834861718664459)
XLA Ops:
  0.6 99.6 %forward0.1 = (f32[2048,3328]{1,0:T(8,128)}, f32[2048,3328]{1,0:T(8,128)}, bf16[2048,3328]{1,0:T(8,128)(2,1)}, bf16[2048,1024]{1,0:T(8,128)(2,1)}, bf16[2,13,102...) custom-call(bf16[2048,1024]{1,0:T(8,128)(2,1)} %bitcast.4, ...), custom_call_target="tpu_custom_call" | custom-call | flops 41875931136 | bytes 68157440 | tf_op jit(solution)/shard_map/forward0/pallas_call | solution.py:244
  100.2 267.4 %backward.1 = (bf16[2,16,13,3,16,128]{5,4,3,2,1,0:T(8,128)(2,1)}, bf16[8,1024,256]{2,1,0:T(8,128)(2,1)}, bf16[8,1024,256]{2,1,0:T(8,128)(2,1)}, bf16[8,256,1024]{2,1,0:T(8,128)(2,1)}) custom-call(bf16[2048,1024]{1,0:T(8,128)(2,1)} %bitcast.5, bf16[2048,1024]{1,0:T(8,128)(2,1)} %get-tuple-element.17.h_ref, bf16[2048,1024]{1,0:T(8,128)(2,1)} %bitcast.6, ...), custom_call_target="tpu_custom_call" | custom-call | flops 167503724544 | bytes 68157440 | tf_op jit(solution)/shard_map/backward/pallas_call | solution.py:505
  367.6 28.3 %update.1 = (bf16[2,128,3328]{2,1,0:T(8,128)(2,1)}, bf16[2,128,3328]{2,1,0:T(8,128)(2,1)}, bf16[2,416,1024]{2,1,0:T(8,128)(2,1)}, f32[2,128,3328]{2,1,0:T(8,128)...) custom-call(bf16[2,16,13,3,16,128]{5,4,3,2,1,0:T(8,128)(2,1)} %get-t, ...), custom_call_target="tpu_custom_call" | custom-call | tf_op jit(solution)/shard_map/update/pallas_call | solution.py:608

commit v4 on v3

v4 whole, which is shorter than its diff:
```python
import functools

import jax
import jax.numpy as jnp
from jax import lax
from jax.experimental import pallas as pl
from jax.experimental.pallas import tpu as pltpu
from jax.sharding import PartitionSpec as P

MESH = pl.DeviceIdType.MESH
f32, bf16 = jnp.float32, jnp.bfloat16
TN = 256
MC = 512
U = 128
VMEM_LIMIT = 67043328


def dot(a, b):
    return lax.dot_general(a, b, (((1,), (0,)), ((), ())), preferred_element_type=f32)


def dot_nt(a, b):
    return lax.dot_general(a, b, (((1,), (1,)), ((), ())), preferred_element_type=f32)


def normed(h):
    wide = h.astype(f32)
    scale = lax.rsqrt(jnp.mean(wide**2, -1, keepdims=True) + 1e-6)
    return (wide * scale).astype(bf16)


def chunks(n, step):
    return [pl.ds(i, step) for i in range(0, n, step)]


class Place:
    def __init__(self):
        self.r, self.s = lax.axis_index("r"), lax.axis_index("s")
        self.y, self.z, self.x, self.c = self.r // 4, self.r % 4, self.s // 2, self.s % 2
        self.peer = (0, self.r, self.s + 1 - 2 * self.c)

    def along(self, dim, d):
        if dim == "y":
            return (0, lax.rem(self.y + d, 4) * 4 + self.z, self.s)
        if dim == "z":
            return (0, self.y * 4 + lax.rem(self.z + d, 4), self.s)
        return (0, self.r, lax.rem(self.x + d, 4) * 2 + self.c)


    def partners(self, along_r):
        some = [self.peer] + [self.along("x", d) for d in (1, 2, 3)]
        if along_r:
            return some + [(0, lax.rem(self.r + d, 16), self.s) for d in range(1, 16)]
        return some + [self.along(dim, d) for dim in "yz" for d in (1, 2, 3)]

    def greet(self, along_r=False):
        barrier = pltpu.get_barrier_semaphore()
        for one in self.partners(along_r):
            pl.semaphore_signal(barrier, inc=1, device_id=one, device_id_type=MESH)

    def greeted(self, along_r=False):
        pl.semaphore_wait(pltpu.get_barrier_semaphore(), len(self.partners(along_r)))


def remote(src, dst, ss, rs, dev):
    return pltpu.make_async_remote_copy(src_ref=src, dst_ref=dst, send_sem=ss, recv_sem=rs, device_id=dev, device_id_type=MESH)


class Fetch:
    A, B, D = 288, 864, 1152

    def __init__(self, place, own, whole, some, sends, recvs):
        self.p, self.own, self.whole, self.some, self.sends, self.recvs = place, own, whole, some, sends, recvs

    def quarters(self, refs, *owner):
        p, (wg, wu, wd) = self.p, refs
        every = (slice(None),)
        return (
            (wg.at[(*owner, pl.ds(32 * p.y, 32))], "y"),
            (wu.at[(*owner, pl.ds(32 * p.z, 32))], "z"),
            (wd.at[(*owner, *every, pl.ds(pl.multiple_of(128 * p.y, 128), 128))], "y"),
            (wd.at[(*owner, *every, pl.ds(pl.multiple_of(512 + 128 * p.z, 128), 128))], "z"),
        )

    def wait(self, rows, sem):
        some = self.some.at[pl.ds(0, rows // 32)]
        pltpu.make_async_copy(some, some, sem).wait()

    def a(self, tile, n):
        src = self.quarters(self.own(tile))
        for d in (1, 2, 3):
            dst = self.quarters(self.whole(tile), 4 - d, self.p.c)
            for (one, _), (other, _) in zip(src, dst, strict=True):
                remote(one, other, self.sends.at[0], self.recvs[0].at[n], self.p.along("x", d)).start()

    def b(self, tile, n):
        self.wait(self.A, self.recvs[0].at[n])
        for ref, dim in self.quarters(self.whole(tile), pl.ds(1, 3), self.p.c):
            for d in (1, 2, 3):
                remote(ref, ref, self.sends.at[1], self.recvs[1].at[n], self.p.along(dim, d)).start()

    def d(self, tile, n):
        self.wait(self.B, self.recvs[1].at[n])
        for whole in self.whole(tile):
            ref = whole.at[pl.ds(1, 3), self.p.c]
            remote(ref, ref, self.sends.at[2], self.recvs[2].at[n], self.p.peer).start()

    def here(self, n):
        self.wait(self.D, self.recvs[2].at[n])

    def sent(self, count):
        def one(_n, _):
            for k, rows in enumerate((self.A, self.B, self.D)):
                self.wait(rows, self.sends.at[k])
            return 0

        lax.fori_loop(0, count, one, 0)


def forward_kernel(tiles, early, x_ref, wg_ref, wu_ref, wd_ref, s_ref, t_ref, p_ref, h_ref, at_ref, wg_all, wu_all, wd_all, some_ref,
                   xv, wg_in, wu_in, wd_in, a, at, acc, wgp, wup, tg, tu, td, isem, osem, orecv, lsem, sends, arecv, brecv, drecv):
    k = pl.program_id(0)
    tokens = x_ref.shape[0]
    place = Place()
    count = tiles + early
    fetch = Fetch(
        place,
        lambda n: (wgp.at[n // tiles, lax.rem(n, tiles)], wup.at[n // tiles, lax.rem(n, tiles)], wd_in.at[n // tiles, lax.rem(n, tiles)]),
        lambda n: (wg_all.at[n // tiles, lax.rem(n, tiles)], wu_all.at[n // tiles, lax.rem(n, tiles)], wd_all.at[n // tiles, lax.rem(n, tiles)]),
        some_ref,
        sends,
        (arecv, brecv, drecv),
    )

    def own_copies(n):
        blocks = (
            (wgp.at[n], wg_all.at[n, :, 0, place.c]),
            (wup.at[n], wu_all.at[n, :, 0, place.c]),
            (wd_in.at[n], wd_all.at[n, :, 0, place.c]),
        )
        here = [pltpu.make_async_copy(src, dst, lsem.at[n, m, 0]) for m, (src, dst) in enumerate(blocks)]
        there = [remote(src, dst, osem.at[n, m], orecv.at[n, m], place.peer) for m, (src, dst) in enumerate(blocks)]
        return here + there

    quarter = lax.broadcasted_iota(jnp.int32, (16, U), 1) // 32

    def permute(n):
        def rows_of(i, _):
            rows = pl.ds(pl.multiple_of(16 * i, 16), 16)
            for src, dst in ((wg_in, wgp), (wu_in, wup)):
                for j in range(tiles):
                    for h in range(2):
                        v = None
                        for o in range(4 * h, 4 * h + 4):
                            one = src[n, rows, pl.ds((416 * o + 32 * j) // U * U, U)]
                            v = one if v is None else jnp.where(quarter == (o + j) % 4, one, v)
                        t = 32 * (j % 4)
                        if t:
                            v = jnp.concatenate([v[:, t:], v[:, :t]], axis=1)
                        dst[n, j, rows, U * h : U * h + U] = v
            return 0

        lax.fori_loop(0, 8, rows_of, 0)

    def loads(tile):
        slot = lax.rem(tile, 2)
        copies = []
        for q, (src, dst) in enumerate(((wg_all, tg), (wu_all, tu), (wd_all, td))):
            for e in range(4):
                copies.append(pltpu.make_async_copy(src.at[0, tile, e], dst.at[slot, lax.rem(place.x + e, 4)], lsem.at[2 + slot, q, e]))
        return copies

    def load(tile):
        fetch.here(tile)
        for cp in loads(tile):
            cp.start()

    def out_at():
        return pltpu.make_async_copy(at, at_ref, isem.at[4])

    @pl.when(k == 0)
    def _():
        place.greet()
        ins = ((wg_ref, wg_in), (wu_ref, wu_in), (wd_ref, wd_in), (x_ref, xv))
        copies = [pltpu.make_async_copy(src, dst, isem.at[n]) for n, (src, dst) in enumerate(ins)]
        for cp in copies:
            cp.start()
        for cp in copies[:3]:
            cp.wait()
        permute(0)
        place.greeted()
        for n in range(3):
            fetch.a(n, n)
        for cp in own_copies(0):
            cp.start()
        for n in range(3, 5):
            fetch.a(n, n)
        copies[3].wait()
        for rows in chunks(tokens, 256):
            a[rows, :] = normed(xv[rows, :])
        fetch.b(0, 0)
        fetch.b(1, 1)
        for rows in chunks(tokens, 256):
            at[:, rows] = a[rows, :].T
        out_at().start()
        fetch.d(0, 0)
        fetch.b(2, 2)
        fetch.b(3, 3)
        for cp in own_copies(0):
            cp.wait()
        load(0)

    @pl.when((k >= 2) & (k < tiles - 1))
    def _():
        load(k + 1)

    @pl.when(k >= 2)
    def _():
        @pl.when(k + 5 < count)
        def _():
            fetch.a(k + 5, k + 5)

        fetch.b(k + 4, k + 4)
        fetch.d(k + 2, k + 2)

    slot = lax.rem(k, 2)
    for cp in loads(k):
        cp.wait()
    wg, wu, wd = tg[slot].reshape(-1, TN), tu[slot].reshape(-1, TN), td[slot].reshape(TN, -1)
    for rows in chunks(tokens, MC):
        g = dot(a[rows, :], wg)
        u = dot(a[rows, :], wu)
        sig = jax.nn.sigmoid(g)
        silu = g * sig
        s_ref[rows, :] = silu
        t_ref[rows, :] = u * (sig * (1 + g * (1 - sig)))
        p_ref[rows, :] = (silu * u).astype(bf16)
    for rows in chunks(tokens, MC):
        acc[rows, :] = jnp.where(k == 0, 0.0, acc[rows, :]) + dot(p_ref[rows, :], wd)

    @pl.when(k == 0)
    def _():
        fetch.d(1, 1)
        fetch.b(4, 4)
        fetch.a(5, 5)
        fetch.d(2, 2)
        load(1)

    @pl.when(k == 1)
    def _():
        fetch.d(3, 3)
        load(2)
        fetch.b(5, 5)
        fetch.a(6, 6)

    @pl.when(k == 2)
    def _():
        permute(1)
        for cp in own_copies(1):
            cp.start()

    @pl.when(k == tiles - 1)
    def _():
        for n in range(tiles + 2, count):
            fetch.d(n, n)
        parts = chunks(tokens, 256)
        out_h = [pltpu.make_async_copy(xv.at[rows, :], h_ref.at[rows, :], isem.at[5 + m]) for m, rows in enumerate(parts)]
        for rows, cp in zip(parts, out_h, strict=True):
            xv[rows, :] = xv[rows, :] + acc[rows, :].astype(bf16)
            cp.start()
        for cp in own_copies(1):
            cp.wait()
        for n in range(tiles, count):
            fetch.here(n)
        fetch.sent(count)
        out_at().wait()
        for cp in out_h:
            cp.wait()


def forward(x, wg, wu, wd, early):
    tokens, d = x.shape
    ff = wg.shape[2]
    tiles = ff // TN
    assert early == 4
    anywhere = pl.BlockSpec(memory_space=pl.ANY)
    hid = pl.BlockSpec((tokens, TN), lambda k: (0, k))
    wd = wd.reshape(2, tiles, 32, d)
    dma = pltpu.SemaphoreType.DMA
    return pl.pallas_call(
        functools.partial(forward_kernel, tiles, early),
        grid=(tiles,),
        in_specs=[anywhere] * 4,
        out_specs=[hid, hid, hid] + [anywhere] * 6,
        out_shape=[jax.ShapeDtypeStruct((tokens, ff), f32)] * 2
        + [jax.ShapeDtypeStruct((tokens, ff), bf16), jax.ShapeDtypeStruct((tokens, d), bf16), jax.ShapeDtypeStruct((d, tokens), bf16)]
        + [jax.ShapeDtypeStruct((2, tiles, 4, 2, 128, TN), bf16)] * 2
        + [jax.ShapeDtypeStruct((2, tiles, 4, 2, 32, d), bf16)]
        + [jax.ShapeDtypeStruct((36, 32, TN), bf16)],
        scratch_shapes=[
            pltpu.VMEM((tokens, d), bf16),
            pltpu.VMEM(wg.shape, bf16),
            pltpu.VMEM(wu.shape, bf16),
            pltpu.VMEM(wd.shape, bf16),
            pltpu.VMEM((tokens, d), bf16),
            pltpu.VMEM((d, tokens), bf16),
            pltpu.VMEM((tokens, d), f32),
            pltpu.VMEM((2, tiles, 128, TN), bf16),
            pltpu.VMEM((2, tiles, 128, TN), bf16),
            pltpu.VMEM((2, 4, 2, 128, TN), bf16),
            pltpu.VMEM((2, 4, 2, 128, TN), bf16),
            pltpu.VMEM((2, 4, 2, 32, d), bf16),
            dma((13,)),
            dma((2, 3)),
            dma((2, 3)),
            dma((4, 3, 4)),
            dma((3,)),
            dma((tiles + early,)),
            dma((tiles + early,)),
            dma((tiles + early,)),
        ],
        compiler_params=pltpu.CompilerParams(vmem_limit_bytes=VMEM_LIMIT, has_side_effects=True, collective_id=1),
        cost_estimate=pl.CostEstimate(flops=6 * tokens * d * ff, bytes_accessed=10 * tokens * ff, transcendentals=0),
        name="forward0",
    )(x, wg, wu, wd)


def backward_kernel(tiles, early, at_ref, h_ref, dy_ref, wg_ref, wu_ref, wd_ref, s_ref, t_ref, p_ref,
                    sums_ref, wg_more, wu_more, wd_more, some_ref,
                    a, at, dy, accg, accu, pbuf, dg, du, tg, tu, td, dgu, dwd, r0gu, r0wd, s1, r1, s2, r2, s3, r3, fin, held,
                    lsem, tsem, s0s, s0r, s1s, s1r, s2s, s2r, s3s, s3r, ags, agr, hs, hr, sends, arecv, brecv, drecv):
    i = pl.program_id(0)
    tokens = a.shape[0]
    place = Place()
    r, c = place.r, place.c
    total = 2 * tiles
    where = {"x": place.x, "y": place.y, "z": place.z}
    ORDER = ("yzx", "zxy", "xyz")

    def stage0(tile):
        slot = lax.rem(tile, 2)
        return [
            remote(dgu.at[slot, :, :, 1 - c], r0gu.at[slot], s0s.at[slot, 0], s0r.at[slot, 0], place.peer),
            remote(dwd.at[slot, :, 1 - c], r0wd.at[slot], s0s.at[slot, 1], s0r.at[slot, 1], place.peer),
        ]

    STAGES = ((s1, r1, s1s, s1r, 2, 4), (s2, r2, s2s, s2r, 2, 4), (s3, r3, s3s, s3r, 2, 4))

    def exchange(n, tile):
        src, dst, ss, rs, held, slots = STAGES[n]
        own, slot = lax.rem(tile, held), lax.rem(tile, slots)
        for q in range(3):
            dim = ORDER[q][n]
            for d in (1, 2, 3):
                part = src.at[own, q, lax.rem(where[dim] + d, 4)]
                remote(part, dst.at[slot, q, d - 1], ss.at[own], rs.at[slot], place.along(dim, d)).start()

    def arrived(n, tile):
        src, dst, ss, rs, held, slots = STAGES[n]
        own, slot = lax.rem(tile, held), lax.rem(tile, slots)
        sent = src.at[own, :, pl.ds(0, 3)]
        pltpu.make_async_copy(sent, sent, ss.at[own]).wait()
        pltpu.make_async_copy(dst.at[slot], dst.at[slot], rs.at[slot]).wait()

    def added(n, tile, q):
        src, dst, _ss, _rs, held, slots = STAGES[n]
        slot = lax.rem(tile, slots)
        own = src[lax.rem(tile, held), q, where[ORDER[q][n]]].astype(f32)
        return (own + dst[slot, q, 0].astype(f32) + dst[slot, q, 1].astype(f32) + dst[slot, q, 2].astype(f32)).astype(bf16)

    fetch = Fetch(
        place,
        lambda j: tuple(w.at[1, j, 0, place.c] for w in (wg_ref, wu_ref, wd_ref)),
        lambda j: (wg_more.at[j - early], wu_more.at[j - early], wd_more.at[j - early]),
        some_ref,
        sends,
        (arecv, brecv, drecv),
    )

    def load(tile, act):
        slot = lax.rem(tile, 2)
        for own, some in ((tile < early, lambda w, _more, e: w.at[1, tile, e]), (tile >= early, lambda w, more, e: more.at[tile - early, e] if e else w.at[1, tile, e])):

            @pl.when(own)
            def _(some=some):
                for q, (w, more, dst) in enumerate(((wg_ref, wg_more, tg), (wu_ref, wu_more, tu), (wd_ref, wd_more, td))):
                    for e in range(4):
                        act(pltpu.make_async_copy(some(w, more, e), dst.at[slot, lax.rem(place.x + e, 4)], tsem.at[slot, q, e]))

    def load0(tile, act):
        slot = lax.rem(tile, 2)
        for e in range(4):
            act(pltpu.make_async_copy(wd_ref.at[0, tile - tiles, e], td.at[slot, lax.rem(place.x + e, 4)], tsem.at[slot, 2, e]))

    @pl.when(i == 0)
    def _():
        place.greet(True)
        cp = [pltpu.make_async_copy(h_ref, a, lsem.at[0]), pltpu.make_async_copy(dy_ref, dy, lsem.at[1])]
        cp[0].start()
        cp[1].start()
        load(i, lambda cp: cp.start())
        cp[0].wait()
        for rows in chunks(tokens, 256):
            v = normed(a[rows, :])
            a[rows, :] = v
            at[:, rows] = v.T
        cp[1].wait()
        place.greeted(True)
        fetch.a(early, 0)

    @pl.when((i >= early - 1) & (i < tiles - 1))
    def _():
        fetch.here(i + 1 - early)

    @pl.when(i < tiles - 1)
    def _():
        load(i + 1, lambda cp: cp.start())

    @pl.when((i >= tiles - 1) & (i < total - 1))
    def _():
        load0(i + 1, lambda cp: cp.start())

    def by_weights(p):
        slot = lax.rem(i, 2)
        for q, one in ((0, dg), (1, du)):
            dgu[slot, q] = dot(at[...], one[...]).astype(bf16).reshape(dgu.shape[2:])
        dwd[slot] = dot(p[...].T, dy[...]).astype(bf16).reshape(dwd.shape[1:])

    @pl.when(i < tiles)
    def _():
        slot = lax.rem(i, 2)
        load(i, lambda cp: cp.wait())
        wg, wu, wd = tg[slot].reshape(-1, TN), tu[slot].reshape(-1, TN), td[slot].reshape(TN, -1)
        for rows in chunks(tokens, MC):
            g = dot(a[rows, :], wg)
            u = dot(a[rows, :], wu)
            d = dot_nt(dy[rows, :], wd).astype(bf16).astype(f32)
            sig = jax.nn.sigmoid(g)
            silu = g * sig
            pbuf[rows, :] = (silu * u).astype(bf16)
            du[rows, :] = (d * silu).astype(bf16)
            dg[rows, :] = (d * u * (sig * (1 + g * (1 - sig)))).astype(bf16)
        for rows in chunks(tokens, MC):
            accg[rows, :] = jnp.where(i == 0, 0.0, accg[rows, :]) + dot_nt(dg[rows, :], wg)
            accu[rows, :] = jnp.where(i == 0, 0.0, accu[rows, :]) + dot_nt(du[rows, :], wu)
        by_weights(pbuf)

    @pl.when((i >= tiles) & (i < total))
    def _():
        load0(i, lambda cp: cp.wait())
        wd = td[lax.rem(i, 2)].reshape(TN, -1)
        for rows in chunks(tokens, MC):
            d = dot_nt(dy[rows, :], wd).astype(bf16).astype(f32)
            du[rows, :] = (d * s_ref[rows, :]).astype(bf16)
            dg[rows, :] = (d * t_ref[rows, :]).astype(bf16)
        by_weights(p_ref)

    @pl.when(i == tiles - 1)
    def _():
        pltpu.make_async_copy(h_ref, a, lsem.at[0]).start()

    def spread(tile):
        layer, j = 1 - tile // tiles, lax.rem(tile, tiles)
        src, dst = fin.at[tile], sums_ref.at[layer, place.y, place.z, j]
        pltpu.make_async_copy(src, dst, agr.at[0]).start()

        def one(d, _):
            to = lax.rem(r + d, 16)
            remote(src, dst, ags.at[0], agr.at[0], (0, to, place.s)).start()
            return 0

        lax.fori_loop(1, 16, one, 0)

    def first_half(tile):
        slot = lax.rem(tile, 4)
        for k, dim in enumerate("yz"):

            @pl.when(lax.rem(tile, 2) == k)
            def _(k=k, dim=dim):
                me = where[dim]
                for q in range(3):
                    held[slot, me, q] = fin[tile, q]
                for d in (1, 2, 3):
                    remote(fin.at[tile], held.at[slot, me], hs.at[k], hr.at[slot], place.along(dim, d)).start()

    def passed_on():
        pltpu.make_async_copy(held.at[0], held.at[0], hs.at[2]).wait()
        pltpu.make_async_copy(held.at[pl.ds(0, 3)], held.at[pl.ds(0, 3)], hs.at[3]).wait()

    def second_half(tile):
        layer, j, slot = 1 - tile // tiles, lax.rem(tile, tiles), lax.rem(tile, 4)
        three = held.at[slot, pl.ds(0, 3)]
        pltpu.make_async_copy(three, three, hr.at[slot]).wait()
        pltpu.make_async_copy(three, three, hs.at[lax.rem(tile, 2)]).wait()

        @pl.when(tile > 0)
        def _():
            passed_on()

        for k, dim in enumerate("yz"):

            @pl.when(lax.rem(tile, 2) == k)
            def _(dim=dim):
                other = "z" if dim == "y" else "y"
                dst = sums_ref.at[layer, :, place.z, j] if dim == "y" else sums_ref.at[layer, place.y, :, j]
                pltpu.make_async_copy(held.at[slot], dst, hs.at[2]).start()
                for d in (1, 2, 3):
                    remote(held.at[slot], dst, hs.at[3], agr.at[0], place.along(other, d)).start()

    def stage4(tile):
        arrived(2, tile)
        for q in range(3):
            fin[tile, q] = added(2, tile, q)

        @pl.when(tile < total - 2)
        def _():
            first_half(tile)

        @pl.when(tile >= total - 2)
        def _():
            spread(tile)

    def stage3(tile):
        arrived(1, tile)
        for q in range(3):
            s3[lax.rem(tile, 2), q] = added(1, tile, q)
        exchange(2, tile)

    def stage2(tile):
        arrived(0, tile)
        for q in range(3):
            s2[lax.rem(tile, 2), q] = added(0, tile, q)
        exchange(1, tile)

    for stage, lag in ((stage4, 5), (stage3, 4), (stage2, 3)):
        end = total + lag - 1

        def steps(first, stage=stage, lag=lag, end=end):
            count = jnp.where(first == end - 1, 2, 1)

            def one(n, _):
                stage(first - lag + n)
                return 0

            lax.fori_loop(0, count, one, 0)

        @pl.when((i >= lag) & (i < end))
        def _(steps=steps):
            steps(i)

    @pl.when((i >= 1) & (i < total + 1))
    def _():
        tile = i - 1
        slot = lax.rem(tile, 2)
        for cp in stage0(tile):
            cp.wait()
        for xi in range(4):
            for k in range(8):
                for h in range(2):
                    rows, cols = pl.ds(16 * k, 16), pl.ds(U * h, U)
                    yi, zi = k // 2, 2 * (k % 2) + h
                    for q, at_ in ((0, (yi, zi, xi)), (1, (zi, xi, yi))):
                        v = dgu[slot, q, xi, c, rows, cols].astype(f32) + r0gu[slot, q, xi, rows, cols].astype(f32)
                        s1[(slot, q, *at_)] = v.astype(bf16)
                    rows, cols = pl.ds(16 * (yi // 2), 16), pl.ds(U * (4 * (yi % 2) + zi), U)
                    v = dwd[slot, xi, c, rows, cols].astype(f32) + r0wd[slot, xi, rows, cols].astype(f32)
                    s1[slot, 2, xi, yi, zi] = v.astype(bf16)
        exchange(0, tile)

    @pl.when(i < total)
    def _():
        for cp in stage0(i):
            cp.start()

    @pl.when(i == 0)
    def _():
        for tile in range(early + 1, tiles):
            fetch.a(tile, tile - early)

    @pl.when((i + 3 >= early) & (i + 3 < tiles))
    def _():
        fetch.d(i + 3, i + 3 - early)

    @pl.when((i + 4 >= early) & (i + 4 < tiles))
    def _():
        fetch.b(i + 4, i + 4 - early)

    @pl.when((i >= 6) & (i < total + 4))
    def _():
        second_half(i - 6)

    @pl.when(i == tiles - 1)
    def _():
        pltpu.make_async_copy(h_ref, a, lsem.at[0]).wait()
        new_at = pltpu.make_async_copy(at_ref, at, lsem.at[1])
        new_at.start()

        def some(k, _):
            rows = pl.ds(pl.multiple_of(32 * k, 32), 32)
            da = (accg[rows, :].astype(bf16) + accu[rows, :].astype(bf16)).astype(f32)
            wide = a[rows, :].astype(f32)
            scale = lax.rsqrt(jnp.mean(wide**2, -1, keepdims=True) + 1e-6)
            along = jnp.sum(da * wide, -1, keepdims=True)
            by_h = da * scale - wide * (along * (scale * scale * scale) * (1.0 / wide.shape[-1]))
            dy[rows, :] = dy[rows, :] + by_h.astype(bf16)
            return 0

        lax.fori_loop(0, tokens // 32, some, 0, unroll=4)
        new_at.wait()

    @pl.when(i == total + 3)
    def _():
        fetch.sent(tiles - early)
        passed_on()
        for units, sem in ((2 * 15 * 3, ags.at[0]), ((total - 2) * 36 + 2 * 48, agr.at[0])):
            some = some_ref.at[pl.ds(0, units // 4)] if units % 4 == 0 else some_ref.at[pl.ds(0, units // 2), pl.ds(0, 16)]
            pltpu.make_async_copy(some, some, sem).wait()


def backward(at, h, dy, wg, wu, wd, s, t, p, early):
    tokens, d = h.shape
    ff = s.shape[1]
    tiles = ff // TN
    last = tiles - 1
    anywhere = pl.BlockSpec(memory_space=pl.ANY)
    clamp = lambda i: jnp.clip(i - tiles, 0, last)
    hid = pl.BlockSpec((tokens, TN), lambda i: (0, clamp(i)))
    dma = pltpu.SemaphoreType.DMA
    unit = (16, U)
    return pl.pallas_call(
        functools.partial(backward_kernel, tiles, early),
        grid=(2 * tiles + 4,),
        in_specs=[anywhere] * 6 + [hid] * 3,
        out_specs=[anywhere] * 5,
        out_shape=[
            jax.ShapeDtypeStruct((2, 4, 4, tiles, 3, *unit), bf16),
            jax.ShapeDtypeStruct((tiles - early, 4, 2, 128, TN), bf16),
            jax.ShapeDtypeStruct((tiles - early, 4, 2, 128, TN), bf16),
            jax.ShapeDtypeStruct((tiles - early, 4, 2, 32, d), bf16),
            jax.ShapeDtypeStruct((240, 32, TN), bf16),
        ],
        scratch_shapes=[
            pltpu.VMEM((tokens, d), bf16),
            pltpu.VMEM((d, tokens), bf16),
            pltpu.VMEM((tokens, d), bf16),
            pltpu.VMEM((tokens, d), f32),
            pltpu.VMEM((tokens, d), f32),
            pltpu.VMEM((tokens, TN), bf16),
            pltpu.VMEM((tokens, TN), bf16),
            pltpu.VMEM((tokens, TN), bf16),
            pltpu.VMEM((2, 4, 2, 128, TN), bf16),
            pltpu.VMEM((2, 4, 2, 128, TN), bf16),
            pltpu.VMEM((2, 4, 2, 32, d), bf16),
            pltpu.VMEM((2, 2, 4, 2, 128, TN), bf16),
            pltpu.VMEM((2, 4, 2, 32, d), bf16),
            pltpu.VMEM((2, 2, 4, 128, TN), bf16),
            pltpu.VMEM((2, 4, 32, d), bf16),
            pltpu.VMEM((2, 3, 4, 4, 4, *unit), bf16),
            pltpu.VMEM((4, 3, 3, 4, 4, *unit), bf16),
            pltpu.VMEM((2, 3, 4, 4, *unit), bf16),
            pltpu.VMEM((4, 3, 3, 4, *unit), bf16),
            pltpu.VMEM((2, 3, 4, *unit), bf16),
            pltpu.VMEM((4, 3, 3, *unit), bf16),
            pltpu.VMEM((2 * tiles, 3, *unit), bf16),
            pltpu.VMEM((4, 4, 3, *unit), bf16),
            dma((2,)),
            dma((2, 3, 4)),
            dma((2, 2)),
            dma((2, 2)),
            dma((2,)),
            dma((4,)),
            dma((2,)),
            dma((4,)),
            dma((2,)),
            dma((4,)),
            dma((1,)),
            dma((1,)),
            dma((4,)),
            dma((4,)),
            dma((3,)),
            dma((tiles - early,)),
            dma((tiles - early,)),
            dma((tiles - early,)),
        ],
        compiler_params=pltpu.CompilerParams(vmem_limit_bytes=VMEM_LIMIT, has_side_effects=True, collective_id=2),
        cost_estimate=pl.CostEstimate(flops=24 * tokens * d * ff, bytes_accessed=10 * tokens * ff, transcendentals=0),
        name="backward",
    )(at, h, dy, wg, wu, wd, s, t, p)[0]


def adamw(w, m, v, g):
    m = 0.9 * m + 0.1 * g
    v = 0.95 * v + 0.05 * g * g
    step = m * lax.rsqrt(v + 1e-8) + 0.1 * w
    return (w - 0.02 * step).astype(bf16), m, v


ROWS = 64


def update_kernel(tiles, steps, sgu_ref, sd_ref, *refs):
    ins, outs = refs[:9], refs[9:]
    i = pl.program_id(0)

    def one(q, at_, g):
        new = adamw(ins[q][at_].astype(f32), ins[3 + q][at_], ins[6 + q][at_], g.astype(f32))
        for n, value in enumerate(new):
            outs[3 * n + q][at_] = value

    @pl.when(i < steps)
    def _():
        def some(t, _):
            rows = pl.ds(pl.multiple_of(16 * t, 16), 16)
            for q in range(2):
                for n in range(2 * tiles):
                    parts = []
                    for k in range(4 * n, 4 * n + 4):
                        owner, j = k // tiles, k % tiles
                        parts.append(sgu_ref[0, 2 * t + owner // 4, j, q, :, 32 * (owner % 4) : 32 * (owner % 4) + 32])
                    one(q, (0, rows, pl.ds(U * n, U)), jnp.concatenate(parts, axis=1))
            return 0

        lax.fori_loop(0, ROWS // 16, some, 0)

    @pl.when(i >= steps)
    def _():
        def tile(j, _):
            for k in range(2):
                for h in range(8):
                    at_ = (0, pl.ds(pl.multiple_of(32 * j + 16 * k, 16), 16), pl.ds(U * h, U))
                    one(2, at_, sd_ref[0, 8 * k + h, j, 0])
            return 0

        lax.fori_loop(0, tiles, tile, 0)


def update(sums, weights, m, v):
    layers, rows, ff = weights[0].shape
    tiles = ff // TN
    each = rows // ROWS
    steps = layers * each
    here = lambda i: (jnp.minimum(i, steps - 1) // each, jnp.minimum(i, steps - 1) % each)
    gu = pl.BlockSpec((1, ROWS, ff), lambda i: (*here(i), 0))
    down = lambda i: jnp.maximum(i - steps, 0)
    wd = pl.BlockSpec((1, *weights[2].shape[1:]), lambda i: (down(i), 0, 0))
    specs = [gu, gu, wd] * 3
    arrays = (*weights, *m, *v)
    return pl.pallas_call(
        functools.partial(update_kernel, tiles, steps),
        grid=(steps + layers,),
        in_specs=[
            pl.BlockSpec((1, ROWS // 8, tiles, 3, 16, U), lambda i: (*here(i), 0, 0, 0, 0)),
            pl.BlockSpec((1, 16, tiles, 1, 16, U), lambda i: (down(i), 0, 0, 2, 0, 0)),
        ]
        + specs,
        out_specs=specs,
        out_shape=[jax.ShapeDtypeStruct(one.shape, one.dtype) for one in arrays],
        compiler_params=pltpu.CompilerParams(vmem_limit_bytes=VMEM_LIMIT),
        name="update",
    )(sums, sums, *arrays)


def solution(mesh):
    def step(x, dy, *arrays):
        weights, m, v = (arrays[i : i + 3] for i in (0, 3, 6))
        early = 4
        s, t, p, h, at, *whole, _ = forward(x[0], *weights, early)
        sums = backward(at, h, dy[0], *whole, s, t, p, early)
        sums = sums.reshape(2, 16, *sums.shape[3:])
        return tuple(update(sums, weights, m, v))

    states, cut = P(("rep", "r", "s"), None, None), P(None, "s", None)
    return jax.shard_map(
        step,
        mesh=mesh,
        in_specs=(states, states) + (cut,) * 9,
        out_specs=(P("rep", "s", None),) * 9,
        check_vma=False,
    )
```

time: 397 us -> 367 us (0.924)
  Pallas kernels: 395 us -> 366 us
    pallas_call x1, Pallas kernels: 267 us -> 248 us  [backward(): pl.pallas_call(functools.partial(backward_kernel, tiles, early), grid=(2...]
    pallas_call x1, Pallas kernels: 28.3 us -> 22.4 us  [update(): pl.pallas_call(functools.partial(update_kernel, tiles, steps), grid=(step...]
    pallas_call x1, Pallas kernels: 99.6 us -> 95.4 us  [forward(): pl.pallas_call(functools.partial(forward_kernel, tiles, early), grid=(til...]
where the time goes in v4:
time: 367 us
  Pallas kernels  366 us (100%)
    pallas_call x1, Pallas kernels, backward(): pl.pallas_call(functools.partial(backward_kernel, tiles, early), grid=(2...  248 us
    pallas_call x1, Pallas kernels, forward(): pl.pallas_call(functools.partial(forward_kernel, tiles, early), grid=(til...  95.4 us
    pallas_call x1, Pallas kernels, update(): pl.pallas_call(functools.partial(update_kernel, tiles, steps), grid=(step...  22.4 us

profile of v4, /device:TPU:0, one launch (start us, length us, event | category | flops | bytes accessed | tf_op | source)
XLA Modules:
  0.0 367.0 jit_solution(4825538740078361025)
XLA Ops:
  0.6 95.4 %forward0.1 = (f32[2048,3328]{1,0:T(8,128)}, f32[2048,3328]{1,0:T(8,128)}, bf16[2048,3328]{1,0:T(8,128)(2,1)}, bf16[2048,1024]{1,0:T(8,128)(2,1)}, bf16[1024,204...) custom-call(bf16[2048,1024]{1,0:T(8,128)(2,1)} %bitcast.7, ...), custom_call_target="tpu_custom_call" | custom-call | flops 41875931136 | bytes 68157440 | tf_op jit(solution)/shard_map/forward0/pallas_call | solution.py:290
  96.0 248.4 %backward.1 = (bf16[2,4,4,13,3,16,128]{6,5,4,3,2,1,0:T(8,128)(2,1)}, bf16[9,4,2,128,256]{4,3,2,1,0:T(8,128)(2,1)}, bf16[9,4,2,128,256]{4,3,2,1,0:T(8,128)(2,1)},...) custom-call(bf16[1024,2048]{1,0:T(8,128)(2,1)} %get-tuple-element.18.at_ref, ...), custom_call_target="tpu_custom_call" | custom-call | flops 167503724544 | bytes 68157440 | tf_op jit(solution)/shard_map/backward/pallas_call | solution.py:630
  344.4 22.4 %update.1 = (bf16[2,128,3328]{2,1,0:T(8,128)(2,1)}, bf16[2,128,3328]{2,1,0:T(8,128)(2,1)}, bf16[2,416,1024]{2,1,0:T(8,128)(2,1)}, f32[2,128,3328]{2,1,0:T(8,128)...) custom-call(bf16[2,16,13,3,16,128]{5,4,3,2,1,0:T(8,128)(2,1)} %bitca, ...), custom_call_target="tpu_custom_call" | custom-call | tf_op jit(solution)/shard_map/update/pallas_call | solution.py:748

commit v5 on v4

--- a/solution.py
+++ b/solution.py
@@ -67,10 +67,12 @@
 
 
 class Fetch:
-    A, B, D = 288, 864, 1152
-
-    def __init__(self, place, own, whole, some, sends, recvs):
+    A, B = 288, 864
+
+    def __init__(self, place, own, whole, some, sends, recvs, first):
         self.p, self.own, self.whole, self.some, self.sends, self.recvs = place, own, whole, some, sends, recvs
+        self.handed = pl.ds(first, 4 - first)
+        self.D = 384 * (4 - first)
 
     def quarters(self, refs, *owner):
         p, (wg, wu, wd) = self.p, refs
@@ -102,7 +104,7 @@
     def d(self, tile, n):
         self.wait(self.B, self.recvs[1].at[n])
         for whole in self.whole(tile):
-            ref = whole.at[pl.ds(1, 3), self.p.c]
+            ref = whole.at[self.handed, self.p.c]
             remote(ref, ref, self.sends.at[2], self.recvs[2].at[n], self.p.peer).start()
 
     def here(self, n):
@@ -130,17 +132,16 @@
         some_ref,
         sends,
         (arecv, brecv, drecv),
+        0,
     )
 
     def own_copies(n):
-        blocks = (
-            (wgp.at[n], wg_all.at[n, :, 0, place.c]),
-            (wup.at[n], wu_all.at[n, :, 0, place.c]),
-            (wd_in.at[n], wd_all.at[n, :, 0, place.c]),
-        )
-        here = [pltpu.make_async_copy(src, dst, lsem.at[n, m, 0]) for m, (src, dst) in enumerate(blocks)]
-        there = [remote(src, dst, osem.at[n, m], orecv.at[n, m], place.peer) for m, (src, dst) in enumerate(blocks)]
-        return here + there
+        blocks = ((wgp.at[n], wg_all.at[n, :, 0, place.c]), (wup.at[n], wu_all.at[n, :, 0, place.c]), (wd_in.at[n], wd_all.at[n, :, 0, place.c]))
+        copies = [pltpu.make_async_copy(src, dst, lsem.at[n, m, 0]) for m, (src, dst) in enumerate(blocks)]
+        if n == 1:
+            late = pl.ds(early, tiles - early)
+            copies += [remote(src.at[late], dst.at[late], osem.at[m], orecv.at[m], place.peer) for m, (src, dst) in enumerate(blocks)]
+        return copies
 
     quarter = lax.broadcasted_iota(jnp.int32, (16, U), 1) // 32
 
@@ -175,17 +176,23 @@
         for cp in loads(tile):
             cp.start()
 
+    def fetched(n):
+        pairs = ((wg_ref, wg_in), (wu_ref, wu_in), (wd_ref, wd_in))
+        return [pltpu.make_async_copy(src.at[n], dst.at[n], isem.at[13 * n + m]) for m, (src, dst) in enumerate(pairs)]
+
     def out_at():
         return pltpu.make_async_copy(at, at_ref, isem.at[4])
 
     @pl.when(k == 0)
     def _():
         place.greet()
-        ins = ((wg_ref, wg_in), (wu_ref, wu_in), (wd_ref, wd_in), (x_ref, xv))
-        copies = [pltpu.make_async_copy(src, dst, isem.at[n]) for n, (src, dst) in enumerate(ins)]
-        for cp in copies:
+        for cp in fetched(0):
             cp.start()
-        for cp in copies[:3]:
+        get_x = pltpu.make_async_copy(x_ref, xv, isem.at[3])
+        get_x.start()
+        for cp in fetched(1):
+            cp.start()
+        for cp in fetched(0):
             cp.wait()
         permute(0)
         place.greeted()
@@ -195,7 +202,7 @@
             cp.start()
         for n in range(3, 5):
             fetch.a(n, n)
-        copies[3].wait()
+        get_x.wait()
         for rows in chunks(tokens, 256):
             a[rows, :] = normed(xv[rows, :])
         fetch.b(0, 0)
@@ -203,25 +210,29 @@
         for rows in chunks(tokens, 256):
             at[:, rows] = a[rows, :].T
         out_at().start()
+        for cp in own_copies(0):
+            cp.wait()
         fetch.d(0, 0)
         fetch.b(2, 2)
         fetch.b(3, 3)
-        for cp in own_copies(0):
-            cp.wait()
         load(0)
 
     @pl.when((k >= 2) & (k < tiles - 1))
     def _():
         load(k + 1)
 
-    @pl.when(k >= 2)
-    def _():
-        @pl.when(k + 5 < count)
+    def ahead(stage, lead, more):
+        @pl.when((k >= 2) & (k <= more))
         def _():
-            fetch.a(k + 5, k + 5)
-
-        fetch.b(k + 4, k + 4)
-        fetch.d(k + 2, k + 2)
+            stage(k + lead, k + lead)
+
+        @pl.when((k >= more) & (k + lead + 1 < count))
+        def _():
+            stage(k + lead + 1, k + lead + 1)
+
+    ahead(fetch.a, 5, 6)
+    ahead(fetch.b, 4, 8)
+    ahead(fetch.d, 2, 10)
 
     slot = lax.rem(k, 2)
     for cp in loads(k):
@@ -255,21 +266,28 @@
 
     @pl.when(k == 2)
     def _():
+        for cp in fetched(1):
+            cp.wait()
         permute(1)
+
+    @pl.when(k == 6)
+    def _():
         for cp in own_copies(1):
             cp.start()
 
+    @pl.when(k == 8)
+    def _():
+        for cp in own_copies(1):
+            cp.wait()
+
     @pl.when(k == tiles - 1)
     def _():
-        for n in range(tiles + 2, count):
-            fetch.d(n, n)
+        fetch.d(count - 1, count - 1)
         parts = chunks(tokens, 256)
         out_h = [pltpu.make_async_copy(xv.at[rows, :], h_ref.at[rows, :], isem.at[5 + m]) for m, rows in enumerate(parts)]
         for rows, cp in zip(parts, out_h, strict=True):
             xv[rows, :] = xv[rows, :] + acc[rows, :].astype(bf16)
             cp.start()
-        for cp in own_copies(1):
-            cp.wait()
         for n in range(tiles, count):
             fetch.here(n)
         fetch.sent(count)
@@ -296,7 +314,7 @@
         + [jax.ShapeDtypeStruct((tokens, ff), bf16), jax.ShapeDtypeStruct((tokens, d), bf16), jax.ShapeDtypeStruct((d, tokens), bf16)]
         + [jax.ShapeDtypeStruct((2, tiles, 4, 2, 128, TN), bf16)] * 2
         + [jax.ShapeDtypeStruct((2, tiles, 4, 2, 32, d), bf16)]
-        + [jax.ShapeDtypeStruct((36, 32, TN), bf16)],
+        + [jax.ShapeDtypeStruct((48, 32, TN), bf16)],
         scratch_shapes=[
             pltpu.VMEM((tokens, d), bf16),
             pltpu.VMEM(wg.shape, bf16),
@@ -310,9 +328,9 @@
             pltpu.VMEM((2, 4, 2, 128, TN), bf16),
             pltpu.VMEM((2, 4, 2, 128, TN), bf16),
             pltpu.VMEM((2, 4, 2, 32, d), bf16),
-            dma((13,)),
-            dma((2, 3)),
-            dma((2, 3)),
+            dma((16,)),
+            dma((3,)),
+            dma((3,)),
             dma((4, 3, 4)),
             dma((3,)),
             dma((tiles + early,)),
@@ -327,8 +345,8 @@
 
 def backward_kernel(tiles, early, at_ref, h_ref, dy_ref, wg_ref, wu_ref, wd_ref, s_ref, t_ref, p_ref,
                     sums_ref, wg_more, wu_more, wd_more, some_ref,
-                    a, at, dy, accg, accu, pbuf, dg, du, tg, tu, td, dgu, dwd, r0gu, r0wd, s1, r1, s2, r2, s3, r3, fin, held,
-                    lsem, tsem, s0s, s0r, s1s, s1r, s2s, s2r, s3s, s3r, ags, agr, hs, hr, sends, arecv, brecv, drecv):
+                    a, at, dy, accg, accu, pbuf, dg, du, tg, tu, td, sv, tv, pv, dgu, dwd, r0gu, r0wd, s1, r1, s2, r2, s3, r3, fin, held,
+                    lsem, tsem, hsem, s0s, s0r, s1s, s1r, s2s, s2r, s3s, s3r, ags, agr, hs, hr, sends, arecv, brecv, drecv):
     i = pl.program_id(0)
     tokens = a.shape[0]
     place = Place()
@@ -375,6 +393,7 @@
         some_ref,
         sends,
         (arecv, brecv, drecv),
+        1,
     )
 
     def load(tile, act):
@@ -391,20 +410,26 @@
         slot = lax.rem(tile, 2)
         for e in range(4):
             act(pltpu.make_async_copy(wd_ref.at[0, tile - tiles, e], td.at[slot, lax.rem(place.x + e, 4)], tsem.at[slot, 2, e]))
+        cols = pl.ds(pl.multiple_of(TN * (tile - tiles), TN), TN)
+        for q, (src, dst) in enumerate(((s_ref, sv), (t_ref, tv), (p_ref, pv))):
+            act(pltpu.make_async_copy(src.at[:, cols], dst.at[slot], hsem.at[slot, q]))
 
     @pl.when(i == 0)
     def _():
         place.greet(True)
-        cp = [pltpu.make_async_copy(h_ref, a, lsem.at[0]), pltpu.make_async_copy(dy_ref, dy, lsem.at[1])]
-        cp[0].start()
-        cp[1].start()
+        parts = chunks(tokens, 256)
+        copies = [pltpu.make_async_copy(h_ref.at[rows, :], a.at[rows, :], lsem.at[2 + n]) for n, rows in enumerate(parts)]
+        for cp in copies:
+            cp.start()
+        get_dy = pltpu.make_async_copy(dy_ref, dy, lsem.at[1])
+        get_dy.start()
         load(i, lambda cp: cp.start())
-        cp[0].wait()
-        for rows in chunks(tokens, 256):
+        for rows, cp in zip(parts, copies, strict=True):
+            cp.wait()
             v = normed(a[rows, :])
             a[rows, :] = v
             at[:, rows] = v.T
-        cp[1].wait()
+        get_dy.wait()
         place.greeted(True)
         fetch.a(early, 0)
 
@@ -448,12 +473,13 @@
     @pl.when((i >= tiles) & (i < total))
     def _():
         load0(i, lambda cp: cp.wait())
-        wd = td[lax.rem(i, 2)].reshape(TN, -1)
+        slot = lax.rem(i, 2)
+        wd = td[slot].reshape(TN, -1)
         for rows in chunks(tokens, MC):
             d = dot_nt(dy[rows, :], wd).astype(bf16).astype(f32)
-            du[rows, :] = (d * s_ref[rows, :]).astype(bf16)
-            dg[rows, :] = (d * t_ref[rows, :]).astype(bf16)
-        by_weights(p_ref)
+            du[rows, :] = (d * sv[slot, rows, :]).astype(bf16)
+            dg[rows, :] = (d * tv[slot, rows, :]).astype(bf16)
+        by_weights(pv.at[slot])
 
     @pl.when(i == tiles - 1)
     def _():
@@ -472,7 +498,7 @@
         lax.fori_loop(1, 16, one, 0)
 
     def first_half(tile):
-        slot = lax.rem(tile, 4)
+        slot = lax.rem(tile, 8)
         for k, dim in enumerate("yz"):
 
             @pl.when(lax.rem(tile, 2) == k)
@@ -483,29 +509,29 @@
                 for d in (1, 2, 3):
                     remote(fin.at[tile], held.at[slot, me], hs.at[k], hr.at[slot], place.along(dim, d)).start()
 
-    def passed_on():
-        pltpu.make_async_copy(held.at[0], held.at[0], hs.at[2]).wait()
-        pltpu.make_async_copy(held.at[pl.ds(0, 3)], held.at[pl.ds(0, 3)], hs.at[3]).wait()
+    def passed_on(tile):
+        pltpu.make_async_copy(held.at[0], held.at[0], hs.at[2 + lax.rem(tile, 2)]).wait()
+        pltpu.make_async_copy(held.at[pl.ds(0, 3)], held.at[pl.ds(0, 3)], hs.at[4 + lax.rem(tile, 2)]).wait()
 
     def second_half(tile):
-        layer, j, slot = 1 - tile // tiles, lax.rem(tile, tiles), lax.rem(tile, 4)
+        layer, j, slot = 1 - tile // tiles, lax.rem(tile, tiles), lax.rem(tile, 8)
         three = held.at[slot, pl.ds(0, 3)]
         pltpu.make_async_copy(three, three, hr.at[slot]).wait()
         pltpu.make_async_copy(three, three, hs.at[lax.rem(tile, 2)]).wait()
 
-        @pl.when(tile > 0)
+        @pl.when(tile > 1)
         def _():
-            passed_on()
+            passed_on(tile - 2)
 
         for k, dim in enumerate("yz"):
 
             @pl.when(lax.rem(tile, 2) == k)
-            def _(dim=dim):
+            def _(k=k, dim=dim):
                 other = "z" if dim == "y" else "y"
                 dst = sums_ref.at[layer, :, place.z, j] if dim == "y" else sums_ref.at[layer, place.y, :, j]
-                pltpu.make_async_copy(held.at[slot], dst, hs.at[2]).start()
+                pltpu.make_async_copy(held.at[slot], dst, hs.at[2 + k]).start()
                 for d in (1, 2, 3):
-                    remote(held.at[slot], dst, hs.at[3], agr.at[0], place.along(other, d)).start()
+                    remote(held.at[slot], dst, hs.at[4 + k], agr.at[0], place.along(other, d)).start()
 
     def stage4(tile):
         arrived(2, tile)
@@ -611,7 +637,8 @@
     @pl.when(i == total + 3)
     def _():
         fetch.sent(tiles - early)
-        passed_on()
+        passed_on(total - 4)
+        passed_on(total - 3)
         for units, sem in ((2 * 15 * 3, ags.at[0]), ((total - 2) * 36 + 2 * 48, agr.at[0])):
             some = some_ref.at[pl.ds(0, units // 4)] if units % 4 == 0 else some_ref.at[pl.ds(0, units // 2), pl.ds(0, 16)]
             pltpu.make_async_copy(some, some, sem).wait()
@@ -621,16 +648,13 @@
     tokens, d = h.shape
     ff = s.shape[1]
     tiles = ff // TN
-    last = tiles - 1
     anywhere = pl.BlockSpec(memory_space=pl.ANY)
-    clamp = lambda i: jnp.clip(i - tiles, 0, last)
-    hid = pl.BlockSpec((tokens, TN), lambda i: (0, clamp(i)))
     dma = pltpu.SemaphoreType.DMA
     unit = (16, U)
     return pl.pallas_call(
         functools.partial(backward_kernel, tiles, early),
         grid=(2 * tiles + 4,),
-        in_specs=[anywhere] * 6 + [hid] * 3,
+        in_specs=[anywhere] * 9,
         out_specs=[anywhere] * 5,
         out_shape=[
             jax.ShapeDtypeStruct((2, 4, 4, tiles, 3, *unit), bf16),
@@ -651,6 +675,9 @@
             pltpu.VMEM((2, 4, 2, 128, TN), bf16),
             pltpu.VMEM((2, 4, 2, 128, TN), bf16),
             pltpu.VMEM((2, 4, 2, 32, d), bf16),
+            pltpu.VMEM((2, tokens, TN), f32),
+            pltpu.VMEM((2, tokens, TN), f32),
+            pltpu.VMEM((2, tokens, TN), bf16),
             pltpu.VMEM((2, 2, 4, 2, 128, TN), bf16),
             pltpu.VMEM((2, 4, 2, 32, d), bf16),
             pltpu.VMEM((2, 2, 4, 128, TN), bf16),
@@ -662,9 +689,10 @@
             pltpu.VMEM((2, 3, 4, *unit), bf16),
             pltpu.VMEM((4, 3, 3, *unit), bf16),
             pltpu.VMEM((2 * tiles, 3, *unit), bf16),
-            pltpu.VMEM((4, 4, 3, *unit), bf16),
-            dma((2,)),
+            pltpu.VMEM((8, 4, 3, *unit), bf16),
+            dma((10,)),
             dma((2, 3, 4)),
+            dma((2, 3)),
             dma((2, 2)),
             dma((2, 2)),
             dma((2,)),
@@ -675,8 +703,8 @@
             dma((4,)),
             dma((1,)),
             dma((1,)),
-            dma((4,)),
-            dma((4,)),
+            dma((6,)),
+            dma((8,)),
             dma((3,)),
             dma((tiles - early,)),
             dma((tiles - early,)),

time: 367 us -> 360 us (0.981)
  Pallas kernels: 366 us -> 359 us
    pallas_call x1, Pallas kernels: 248 us -> 244 us  [backward(): pl.pallas_call(functools.partial(backward_kernel, tiles, early), grid=(2...]
where the time goes in v5:
time: 360 us; the launch traced here: 359 us
  Pallas kernels  359 us (100%)
    pallas_call x1, Pallas kernels, backward(): pl.pallas_call(functools.partial(backward_kernel, tiles, early), grid=(2...  244 us
    pallas_call x1, Pallas kernels, forward(): pl.pallas_call(functools.partial(forward_kernel, tiles, early), grid=(til...  92.5 us
    pallas_call x1, Pallas kernels, update(): pl.pallas_call(functools.partial(update_kernel, tiles, steps), grid=(step...  22.4 us

profile of v5, /device:TPU:0, one launch (start us, length us, event | category | flops | bytes accessed | tf_op | source)
XLA Modules:
  0.0 359.4 jit_solution(18361438893956931935)
XLA Ops:
  0.6 92.5 %forward0.1 = (f32[2048,3328]{1,0:T(8,128)}, f32[2048,3328]{1,0:T(8,128)}, bf16[2048,3328]{1,0:T(8,128)(2,1)}, bf16[2048,1024]{1,0:T(8,128)(2,1)}, bf16[1024,204...) custom-call(bf16[2048,1024]{1,0:T(8,128)(2,1)} %bitcast.7, ...), custom_call_target="tpu_custom_call" | custom-call | flops 41875931136 | bytes 68157440 | tf_op jit(solution)/shard_map/forward0/pallas_call | solution.py:308
  93.2 243.7 %backward.1 = (bf16[2,4,4,13,3,16,128]{6,5,4,3,2,1,0:T(8,128)(2,1)}, bf16[9,4,2,128,256]{4,3,2,1,0:T(8,128)(2,1)}, bf16[9,4,2,128,256]{4,3,2,1,0:T(8,128)(2,1)},...) custom-call(bf16[1024,2048]{1,0:T(8,128)(2,1)} %get-tuple-element.18.at_ref, ...), custom_call_target="tpu_custom_call" | custom-call | flops 167503724544 | bytes 68157440 | tf_op jit(solution)/shard_map/backward/pallas_call | solution.py:654
  336.9 22.4 %update.1 = (bf16[2,128,3328]{2,1,0:T(8,128)(2,1)}, bf16[2,128,3328]{2,1,0:T(8,128)(2,1)}, bf16[2,416,1024]{2,1,0:T(8,128)(2,1)}, f32[2,128,3328]{2,1,0:T(8,128)...) custom-call(bf16[2,16,13,3,16,128]{5,4,3,2,1,0:T(8,128)(2,1)} %bitca, ...), custom_call_target="tpu_custom_call" | custom-call | tf_op jit(solution)/shard_map/update/pallas_call | solution.py:776

commit v6 on v5

--- a/solution.py
+++ b/solution.py
@@ -119,8 +119,8 @@
         lax.fori_loop(0, count, one, 0)
 
 
-def forward_kernel(tiles, early, x_ref, wg_ref, wu_ref, wd_ref, s_ref, t_ref, p_ref, h_ref, at_ref, wg_all, wu_all, wd_all, some_ref,
-                   xv, wg_in, wu_in, wd_in, a, at, acc, wgp, wup, tg, tu, td, isem, osem, orecv, lsem, sends, arecv, brecv, drecv):
+def forward_kernel(tiles, early, x_ref, wg_ref, wu_ref, wd_ref, s_out, t_out, p_out, h_ref, at_ref, wg_all, wu_all, wd_all, some_ref,
+                   xv, wg_in, wu_in, wd_in, a, at, acc, wgp, wup, tg, tu, td, sv, tv, pv, ksem, isem, osem, orecv, lsem, sends, arecv, brecv, drecv):
     k = pl.program_id(0)
     tokens = x_ref.shape[0]
     place = Place()
@@ -237,17 +237,30 @@
     slot = lax.rem(k, 2)
     for cp in loads(k):
         cp.wait()
+    def keep(tile):
+        slot = lax.rem(tile, 2)
+        cols = pl.ds(pl.multiple_of(TN * tile, TN), TN)
+        pairs = ((sv, s_out), (tv, t_out), (pv, p_out))
+        return [pltpu.make_async_copy(src.at[slot], dst.at[:, cols], ksem.at[slot, q]) for q, (src, dst) in enumerate(pairs)]
+
+    @pl.when(k >= 2)
+    def _():
+        for cp in keep(k - 2):
+            cp.wait()
+
     wg, wu, wd = tg[slot].reshape(-1, TN), tu[slot].reshape(-1, TN), td[slot].reshape(TN, -1)
     for rows in chunks(tokens, MC):
         g = dot(a[rows, :], wg)
         u = dot(a[rows, :], wu)
         sig = jax.nn.sigmoid(g)
         silu = g * sig
-        s_ref[rows, :] = silu
-        t_ref[rows, :] = u * (sig * (1 + g * (1 - sig)))
-        p_ref[rows, :] = (silu * u).astype(bf16)
+        sv[slot, rows, :] = silu
+        tv[slot, rows, :] = u * (sig * (1 + g * (1 - sig)))
+        pv[slot, rows, :] = (silu * u).astype(bf16)
     for rows in chunks(tokens, MC):
-        acc[rows, :] = jnp.where(k == 0, 0.0, acc[rows, :]) + dot(p_ref[rows, :], wd)
+        acc[rows, :] = jnp.where(k == 0, 0.0, acc[rows, :]) + dot(pv[slot, rows, :], wd)
+    for cp in keep(k):
+        cp.start()
 
     @pl.when(k == 0)
     def _():
@@ -292,7 +305,7 @@
             fetch.here(n)
         fetch.sent(count)
         out_at().wait()
-        for cp in out_h:
+        for cp in out_h + keep(k - 1) + keep(k):
             cp.wait()
 
 
@@ -302,14 +315,13 @@
     tiles = ff // TN
     assert early == 4
     anywhere = pl.BlockSpec(memory_space=pl.ANY)
-    hid = pl.BlockSpec((tokens, TN), lambda k: (0, k))
     wd = wd.reshape(2, tiles, 32, d)
     dma = pltpu.SemaphoreType.DMA
     return pl.pallas_call(
         functools.partial(forward_kernel, tiles, early),
         grid=(tiles,),
         in_specs=[anywhere] * 4,
-        out_specs=[hid, hid, hid] + [anywhere] * 6,
+        out_specs=[anywhere] * 9,
         out_shape=[jax.ShapeDtypeStruct((tokens, ff), f32)] * 2
         + [jax.ShapeDtypeStruct((tokens, ff), bf16), jax.ShapeDtypeStruct((tokens, d), bf16), jax.ShapeDtypeStruct((d, tokens), bf16)]
         + [jax.ShapeDtypeStruct((2, tiles, 4, 2, 128, TN), bf16)] * 2
@@ -328,6 +340,10 @@
             pltpu.VMEM((2, 4, 2, 128, TN), bf16),
             pltpu.VMEM((2, 4, 2, 128, TN), bf16),
             pltpu.VMEM((2, 4, 2, 32, d), bf16),
+            pltpu.VMEM((2, tokens, TN), f32),
+            pltpu.VMEM((2, tokens, TN), f32),
+            pltpu.VMEM((2, tokens, TN), bf16),
+            dma((2, 3)),
             dma((16,)),
             dma((3,)),
             dma((3,)),
@@ -723,7 +739,7 @@
     return (w - 0.02 * step).astype(bf16), m, v
 
 
-ROWS = 64
+ROWS = 128
 
 
 def update_kernel(tiles, steps, sgu_ref, sd_ref, *refs):

time: 360 us -> 354 us (0.983)
  Pallas kernels: 359 us -> 353 us
where the time goes in v6:
time: 354 us
  Pallas kernels  353 us (100%)
    pallas_call x1, Pallas kernels, backward(): pl.pallas_call(functools.partial(backward_kernel, tiles, early), grid=(2...  243 us
    pallas_call x1, Pallas kernels, forward(): pl.pallas_call(functools.partial(forward_kernel, tiles, early), grid=(til...  89.1 us
    pallas_call x1, Pallas kernels, update(): pl.pallas_call(functools.partial(update_kernel, tiles, steps), grid=(step...  21 us

profile of v6, /device:TPU:0, one launch (start us, length us, event | category | flops | bytes accessed | tf_op | source)
XLA Modules:
  0.0 354.3 jit_solution(1853895483180780981)
XLA Ops:
  0.6 89.1 %forward0.1 = (f32[2048,3328]{1,0:T(8,128)}, f32[2048,3328]{1,0:T(8,128)}, bf16[2048,3328]{1,0:T(8,128)(2,1)}, bf16[2048,1024]{1,0:T(8,128)(2,1)}, bf16[1024,204...) custom-call(bf16[2048,1024]{1,0:T(8,128)(2,1)} %bitcast.7, ...), custom_call_target="tpu_custom_call" | custom-call | flops 41875931136 | bytes 68157440 | tf_op jit(solution)/shard_map/forward0/pallas_call | solution.py:320
  89.8 243.4 %backward.1 = (bf16[2,4,4,13,3,16,128]{6,5,4,3,2,1,0:T(8,128)(2,1)}, bf16[9,4,2,128,256]{4,3,2,1,0:T(8,128)(2,1)}, bf16[9,4,2,128,256]{4,3,2,1,0:T(8,128)(2,1)},...) custom-call(bf16[1024,2048]{1,0:T(8,128)(2,1)} %get-tuple-element.18.at_ref, ...), custom_call_target="tpu_custom_call" | custom-call | flops 167503724544 | bytes 68157440 | tf_op jit(solution)/shard_map/backward/pallas_call | solution.py:670
  333.2 21.0 %update.1 = (bf16[2,128,3328]{2,1,0:T(8,128)(2,1)}, bf16[2,128,3328]{2,1,0:T(8,128)(2,1)}, bf16[2,416,1024]{2,1,0:T(8,128)(2,1)}, f32[2,128,3328]{2,1,0:T(8,128)...) custom-call(bf16[2,16,13,3,16,128]{5,4,3,2,1,0:T(8,128)(2,1)} %bitca, ...), custom_call_target="tpu_custom_call" | custom-call | tf_op jit(solution)/shard_map/update/pallas_call | solution.py:792
